TPU v7x, 256 devices: a whole 4x4x8 slice. The times are simulated.
256 devices in a mesh: dp: 4 (over y), tensor: 64 (over x, z, core).
Axes of the slice: x: 4, y: 4, z: 8, core: 2. Of those that a mesh axis runs over, the one named last changes fastest.
Arguments:
- hidden_acts: bfloat16 [3, 1792, 14336], P(None, 'dp', 'tensor'), may hold values from -6 to 6
- out_grads: bfloat16 [3, 1792, 4096], P(None, 'dp', 'tensor'), may hold values from -6 to 6
Outputs:
- fisher: float32 [14336, 4096], P('tensor', 'dp')
All inputs are finite; a program needn't handle non-finite values.
Results may differ from a plain program's by a relative error of at most 0.018.
Values may be sent and summed in bfloat16 or wider, within the bound.
No kernel may reach another device: no remote copies, remote signals or barrier semaphores. Data moves between devices by JAX's collectives and lax.ppermute only.
A program may use at most 64 MiB of HBM per device.

v0:
```python
import math

import jax
import jax.numpy as jnp
import numpy as np
from jax import lax
from jax.sharding import PartitionSpec as P

FF = 14336
FACTOR_A = 28
SEQS = 3


def cut_along(array, dim, count):
    shape = array.shape
    pieces = array.reshape(*shape[:dim], count, shape[dim] // count, *shape[dim + 1 :])
    return jnp.moveaxis(pieces, dim, 0)


def sum_at_owner(array, axis, dim):
    pieces = cut_along(array, dim, lax.axis_size(axis))
    arrived = lax.all_to_all(pieces, axis, split_axis=0, concat_axis=0, tiled=True)
    return arrived.astype(jnp.float32).sum(axis=0)


def sylvester(order):
    result = np.ones((1, 1))
    for doubling in range(order.bit_length() - 1):
        result = np.kron(result, np.array([[1.0, 1.0], [1.0, -1.0]]))
    return result


def paley_matrix():
    residues = set((number * number % 13 for number in range(1, 13)))
    core_table = np.zeros((14, 14))
    core_table[0, 1:] = 1.0
    core_table[1:, 0] = 1.0
    for row_index in range(13):
        for col_index in range(13):
            offset = (col_index - row_index) % 13
            if offset != 0:
                core_table[1 + row_index, 1 + col_index] = 1.0 if offset in residues else -1.0
    return np.kron(core_table, np.array([[1.0, 1.0], [1.0, -1.0]])) + np.kron(
        np.eye(14), np.array([[1.0, -1.0], [-1.0, -1.0]])
    )


def cross_rotate(values, scaling):
    tok_rows, local_ff = values.shape
    tensor_count = lax.axis_size("tensor")
    mixing = jnp.asarray(sylvester(tensor_count), jnp.float32)
    stacked = values.reshape(tok_rows, 1, local_ff)
    spread = lax.all_to_all(
        stacked.astype(jnp.bfloat16), "tensor", split_axis=0, concat_axis=1, tiled=True
    ).astype(stacked.dtype)
    mixed = jnp.einsum("tqc,qp->tpc", spread, mixing, precision=lax.Precision.HIGHEST)
    scaled = (mixed * scaling).astype(jnp.bfloat16)
    returned = lax.all_to_all(scaled, "tensor", split_axis=1, concat_axis=0, tiled=True)
    return returned.reshape(tok_rows, local_ff)


def on_device(hidden_acts, out_grads):
    seq_count, tok_rows, local_ff = hidden_acts.shape
    dp_count = lax.axis_size("dp")
    local_b = local_ff // FACTOR_A
    local_rot = jnp.asarray(np.kron(sylvester(local_b), paley_matrix()), jnp.bfloat16)
    scaling = 1.0 / math.sqrt(FF)
    inv_root = 1.0 / math.sqrt(tok_rows * dp_count)
    fisher = None
    for seq_index in range(seq_count):
        inner = jnp.dot(hidden_acts[seq_index], local_rot, preferred_element_type=jnp.float32)
        rotated = cross_rotate(inner, scaling)
        partial_sum = lax.dot_general(
            rotated,
            lax.all_gather(out_grads[seq_index], "tensor", axis=1, tiled=True),
            (((0,), (0,)), ((), ())),
            preferred_element_type=jnp.float32,
        )
        summed = sum_at_owner(partial_sum.astype(jnp.bfloat16), "dp", 1)
        gradient = summed * inv_root
        fisher = gradient * gradient if fisher is None else fisher + gradient * gradient
    return fisher / SEQS


def solution(mesh):
    placed = (P(None, "dp", "tensor"), P(None, "dp", "tensor"))
    return jax.shard_map(
        on_device, mesh=mesh, in_specs=placed, out_specs=P("tensor", "dp"), check_vma=False
    )
```

profile of v0, /device:TPU:1, one launch (start us, length us, event | category | flops | bytes accessed | tf_op | source)
XLA Modules:
  0.0 298.0 jit_solution(3031981806293739496)
XLA Ops:
  6.5 1.6 fusion.24
  13.6 13.1 %all-to-all-start.6 = ((bf16[64,2,784]{2,1,0:T(2,128)(2,1)}), bf16[64,2,784]{2,1,0:T(2,128)(2,1)S(1)}, u32[]{:S(2)}, u32[]{:S(2)}) async-start(bf16[64,2,784]{2,1,0:T(2,128)(2,1)} %reshape.40), calls=%async_computation.6 | async-start | bytes 458752 | tf_op jit(solution)/shard_map/all_to_all | solution.py:53
  30.1 8.4 %all-to-all-done.6 = bf16[64,2,784]{2,1,0:T(2,128)(2,1)S(1)} async-done(((bf16[64,2,784]{2,1,0:T(2,128)(2,1)}), bf16[64,2,784]{2,1,0:T(2,128)(2,1)S(1)}, u32[]{:S(2)}, u32[]{:S(2)}) %all-to-all-start.6) | async-done | bytes 200736 | tf_op jit(solution)/shard_map/all_to_all | solution.py:53
  38.5 6.3 %all-to-all-start.3 = ((bf16[64,2,784]{2,1,0:T(2,128)(2,1)}), bf16[64,2,784]{2,1,0:T(2,128)(2,1)S(1)}, u32[]{:S(2)}, u32[]{:S(2)}) async-start(bf16[64,2,784]{2,1,0:T(2,128)(2,1)} %reshape.42), calls=%async_computation.3 | async-start | bytes 458752 | tf_op jit(solution)/shard_map/all_to_all | solution.py:53
  48.1 8.3 %all-to-all-done.3 = bf16[64,2,784]{2,1,0:T(2,128)(2,1)S(1)} async-done(((bf16[64,2,784]{2,1,0:T(2,128)(2,1)}), bf16[64,2,784]{2,1,0:T(2,128)(2,1)S(1)}, u32[]{:S(2)}, u32[]{:S(2)}) %all-to-all-start.3) | async-done | bytes 200736 | tf_op jit(solution)/shard_map/all_to_all | solution.py:53
  56.4 6.0 %all-to-all-start = ((bf16[64,2,784]{2,1,0:T(2,128)(2,1)}), bf16[64,2,784]{2,1,0:T(2,128)(2,1)S(1)}, u32[]{:S(2)}, u32[]{:S(2)}) async-start(bf16[64,2,784]{2,1,0:T(2,128)(2,1)} %reshape.44), calls=%async_computation | async-start | bytes 458752 | tf_op jit(solution)/shard_map/all_to_all | solution.py:53
  65.5 9.8 %all-to-all-done = bf16[64,2,784]{2,1,0:T(2,128)(2,1)S(1)} async-done(((bf16[64,2,784]{2,1,0:T(2,128)(2,1)}), bf16[64,2,784]{2,1,0:T(2,128)(2,1)S(1)}, u32[]{:S(2)}, u32[]{:S(2)}) %all-to-all-start) | async-done | bytes 200736 | tf_op jit(solution)/shard_map/all_to_all | solution.py:53
  75.3 6.3 %all-to-all-start.7 = ((bf16[7,64,224]{2,0,1:T(8,128)(2,1)}), bf16[7,64,224]{2,0,1:T(8,128)(2,1)S(1)}, u32[]{:S(2)}, u32[]{:S(2)}) async-start(bf16[7,64,224]{2,0,1:T(8,128)(2,1)} %copy.29), calls=%async_computation.7 | async-start | bytes 524288 | tf_op jit(solution)/shard_map/all_to_all | solution.py:58
  84.7 10.7 %all-to-all-done.7 = bf16[7,64,224]{2,0,1:T(8,128)(2,1)S(1)} async-done(((bf16[7,64,224]{2,0,1:T(8,128)(2,1)}), bf16[7,64,224]{2,0,1:T(8,128)(2,1)S(1)}, u32[]{:S(2)}, u32[]{:S(2)}) %all-to-all-start.7) | async-done | bytes 200736 | tf_op jit(solution)/shard_map/all_to_all | solution.py:58
  95.5 6.4 %all-to-all-start.4 = ((bf16[7,64,224]{2,0,1:T(8,128)(2,1)}), bf16[7,64,224]{2,0,1:T(8,128)(2,1)S(1)}, u32[]{:S(2)}, u32[]{:S(2)}) async-start(bf16[7,64,224]{2,0,1:T(8,128)(2,1)} %copy.25), calls=%async_computation.4 | async-start | bytes 524288 | tf_op jit(solution)/shard_map/all_to_all | solution.py:58
  104.9 8.9 %all-to-all-done.4 = bf16[7,64,224]{2,0,1:T(8,128)(2,1)S(1)} async-done(((bf16[7,64,224]{2,0,1:T(8,128)(2,1)}), bf16[7,64,224]{2,0,1:T(8,128)(2,1)S(1)}, u32[]{:S(2)}, u32[]{:S(2)}) %all-to-all-start.4) | async-done | bytes 200736 | tf_op jit(solution)/shard_map/all_to_all | solution.py:58
  113.8 6.0 %all-to-all-start.1 = ((bf16[7,64,224]{2,0,1:T(8,128)(2,1)}), bf16[7,64,224]{2,0,1:T(8,128)(2,1)S(1)}, u32[]{:S(2)}, u32[]{:S(2)}) async-start(bf16[7,64,224]{2,0,1:T(8,128)(2,1)} %copy.21), calls=%async_computation.1 | async-start | bytes 524288 | tf_op jit(solution)/shard_map/all_to_all | solution.py:58
  120.0 3.7 %convolution_convert_fusion = bf16[224,4096]{1,0:T(8,128)(2,1)S(1)} fusion(bf16[448,224]{1,0:T(8,128)(2,1)S(1)} %reshape.31, bf16[1,448,4096]{1,2,0:T(8,128)(2,1)} %all-gather.11.cloned.1.call-done), kind=kOutput, calls=%fused_computation | convolution fusion | flops 823001088 | bytes 5705728 | tf_op jit(solution)/shard_map/dot_general | solution.py:73
  125.2 7.4 %all-to-all-done.1 = bf16[7,64,224]{2,0,1:T(8,128)(2,1)S(1)} async-done(((bf16[7,64,224]{2,0,1:T(8,128)(2,1)}), bf16[7,64,224]{2,0,1:T(8,128)(2,1)S(1)}, u32[]{:S(2)}, u32[]{:S(2)}) %all-to-all-start.1) | async-done | bytes 200736 | tf_op jit(solution)/shard_map/all_to_all | solution.py:58
  132.5 4.4 %all-to-all-start.8 = ((bf16[4,224,1024]{2,1,0:T(8,128)(2,1)}), bf16[4,224,1024]{2,1,0:T(8,128)(2,1)S(1)}, u32[]{:S(2)}, u32[]{:S(2)}) async-start(bf16[4,224,1024]{2,1,0:T(8,128)(2,1)} %bitcast.92), calls=%async_computation.8 | async-start | bytes 3670016 | tf_op jit(solution)/shard_map/all_to_all | solution.py:22
  137.0 39.4 %all-gather.9.cloned.1.call-done = bf16[1,448,4096]{1,2,0:T(8,128)(2,1)} async-done(((bf16[1,448,64]{1,2,0:T(8,128)(2,1)}), bf16[1,448,4096]{1,2,0:T(8,128)(2,1)}) %all-gather.9.cloned.1.call-update) | async-done | bytes 3670032 | tf_op jit(solution)/shard_map/all_gather | solution.py:75
  176.4 3.7 %convolution_convert_fusion.1 = bf16[224,4096]{1,0:T(8,128)(2,1)S(1)} fusion(bf16[448,224]{1,0:T(8,128)(2,1)S(1)} %reshape.29, bf16[1,448,4096]{1,2,0:T(8,128)(2,1)} %all-gather.9.cloned.1.call-done), kind=kOutput, calls=%fused_computation.1 | convolution fusion | flops 823001088 | bytes 5705728 | tf_op jit(solution)/shard_map/dot_general | solution.py:73
  181.5 4.4 %all-to-all-start.5 = ((bf16[4,224,1024]{2,1,0:T(8,128)(2,1)}), bf16[4,224,1024]{2,1,0:T(8,128)(2,1)}, u32[]{:S(2)}, u32[]{:S(2)}) async-start(bf16[4,224,1024]{2,1,0:T(8,128)(2,1)} %bitcast.94), calls=%async_computation.5 | async-start | bytes 3670016 | tf_op jit(solution)/shard_map/all_to_all | solution.py:22
  186.0 69.3 %all-gather.7.cloned.1.call-done = bf16[1,448,4096]{1,2,0:T(8,128)(2,1)} async-done(((bf16[1,448,64]{1,2,0:T(8,128)(2,1)}), bf16[1,448,4096]{1,2,0:T(8,128)(2,1)}) %all-gather.7.cloned.1.call-update) | async-done | bytes 3670032 | tf_op jit(solution)/shard_map/all_gather | solution.py:75
  255.3 3.6 %convolution_convert_fusion.2 = bf16[224,4096]{1,0:T(8,128)(2,1)S(1)} fusion(bf16[448,224]{1,0:T(8,128)(2,1)S(1)} %reshape.27, bf16[1,448,4096]{1,2,0:T(8,128)(2,1)} %all-gather.7.cloned.1.call-done), kind=kOutput, calls=%fused_computation.2 | convolution fusion | flops 823001088 | bytes 5705728 | tf_op jit(solution)/shard_map/dot_general | solution.py:73
  260.4 4.4 %all-to-all-start.2 = ((bf16[4,224,1024]{2,1,0:T(8,128)(2,1)}), bf16[4,224,1024]{2,1,0:T(8,128)(2,1)}, u32[]{:S(2)}, u32[]{:S(2)}) async-start(bf16[4,224,1024]{2,1,0:T(8,128)(2,1)} %bitcast.96), calls=%async_computation.2 | async-start | bytes 3670016 | tf_op jit(solution)/shard_map/all_to_all | solution.py:22
  265.2 1.9 convert_reduce_fusion.1
  267.1 21.1 %all-to-all-done.2 = bf16[4,224,1024]{2,1,0:T(8,128)(2,1)} async-done(((bf16[4,224,1024]{2,1,0:T(8,128)(2,1)}), bf16[4,224,1024]{2,1,0:T(8,128)(2,1)}, u32[]{:S(2)}, u32[]{:S(2)}) %all-to-all-start.2) | async-done | bytes 1835040 | tf_op jit(solution)/shard_map/all_to_all | solution.py:22
  288.3 1.9 convert_reduce_fusion.2
  (49 shorter events, 27.6 us)
Async XLA Ops:
  6.5 38.3 %copy-start = (bf16[224,224]{1,0:T(8,128)(2,1)S(1)}, bf16[224,224]{1,0:T(8,128)(2,1)}, u32[]{:S(2)}) copy-start(bf16[224,224]{1,0:T(8,128)(2,1)} %constant.13.clone) | copy-start | bytes 301060
  6.5 113.5 %all-gather.11.cloned.1.call-start = ((), (), s32[]{:S(2)}) async-start(), calls=%async_computation.11 | async-start | bytes 4259840 | tf_op jit(solution)/shard_map/all_gather | solution.py:75
  8.2 168.2 %all-gather.9.cloned.1.call-start = ((), (), s32[]{:S(2)}) async-start(), calls=%async_computation.10 | async-start | bytes 4259840 | tf_op jit(solution)/shard_map/all_gather | solution.py:75
  8.9 246.4 %all-gather.7.cloned.1.call-start = ((), (), s32[]{:S(2)}) async-start(), calls=%async_computation.9 | async-start | bytes 4259840 | tf_op jit(solution)/shard_map/all_gather | solution.py:75
  13.6 50.7 %copy-start.1 = (f32[64,64,1]{0,1,2:T(8,128)S(1)}, f32[64,64,1]{0,1,2:T(8,128)}, u32[]{:S(2)}) copy-start(f32[64,64,1]{0,1,2:T(8,128)} %constant.16) | copy-start | bytes 49156
  13.6 24.8 %all-to-all-start.6 = ((bf16[64,2,784]{2,1,0:T(2,128)(2,1)}), bf16[64,2,784]{2,1,0:T(2,128)(2,1)S(1)}, u32[]{:S(2)}, u32[]{:S(2)}) async-start(bf16[64,2,784]{2,1,0:T(2,128)(2,1)} %reshape.40), calls=%async_computation.6 | async-start | bytes 458752 | tf_op jit(solution)/shard_map/all_to_all | solution.py:53
  38.5 17.9 %all-to-all-start.3 = ((bf16[64,2,784]{2,1,0:T(2,128)(2,1)}), bf16[64,2,784]{2,1,0:T(2,128)(2,1)S(1)}, u32[]{:S(2)}, u32[]{:S(2)}) async-start(bf16[64,2,784]{2,1,0:T(2,128)(2,1)} %reshape.42), calls=%async_computation.3 | async-start | bytes 458752 | tf_op jit(solution)/shard_map/all_to_all | solution.py:53
  56.4 18.9 %all-to-all-start = ((bf16[64,2,784]{2,1,0:T(2,128)(2,1)}), bf16[64,2,784]{2,1,0:T(2,128)(2,1)S(1)}, u32[]{:S(2)}, u32[]{:S(2)}) async-start(bf16[64,2,784]{2,1,0:T(2,128)(2,1)} %reshape.44), calls=%async_computation | async-start | bytes 458752 | tf_op jit(solution)/shard_map/all_to_all | solution.py:53
  75.3 20.1 %all-to-all-start.7 = ((bf16[7,64,224]{2,0,1:T(8,128)(2,1)}), bf16[7,64,224]{2,0,1:T(8,128)(2,1)S(1)}, u32[]{:S(2)}, u32[]{:S(2)}) async-start(bf16[7,64,224]{2,0,1:T(8,128)(2,1)} %copy.29), calls=%async_computation.7 | async-start | bytes 524288 | tf_op jit(solution)/shard_map/all_to_all | solution.py:58
  95.5 18.3 %all-to-all-start.4 = ((bf16[7,64,224]{2,0,1:T(8,128)(2,1)}), bf16[7,64,224]{2,0,1:T(8,128)(2,1)S(1)}, u32[]{:S(2)}, u32[]{:S(2)}) async-start(bf16[7,64,224]{2,0,1:T(8,128)(2,1)} %copy.25), calls=%async_computation.4 | async-start | bytes 524288 | tf_op jit(solution)/shard_map/all_to_all | solution.py:58
  113.8 18.7 %all-to-all-start.1 = ((bf16[7,64,224]{2,0,1:T(8,128)(2,1)}), bf16[7,64,224]{2,0,1:T(8,128)(2,1)S(1)}, u32[]{:S(2)}, u32[]{:S(2)}) async-start(bf16[7,64,224]{2,0,1:T(8,128)(2,1)} %copy.21), calls=%async_computation.1 | async-start | bytes 524288 | tf_op jit(solution)/shard_map/all_to_all | solution.py:58
  132.5 49.0 %all-to-all-start.8 = ((bf16[4,224,1024]{2,1,0:T(8,128)(2,1)}), bf16[4,224,1024]{2,1,0:T(8,128)(2,1)S(1)}, u32[]{:S(2)}, u32[]{:S(2)}) async-start(bf16[4,224,1024]{2,1,0:T(8,128)(2,1)} %bitcast.92), calls=%async_computation.8 | async-start | bytes 3670016 | tf_op jit(solution)/shard_map/all_to_all | solution.py:22
  181.5 78.9 %all-to-all-start.5 = ((bf16[4,224,1024]{2,1,0:T(8,128)(2,1)}), bf16[4,224,1024]{2,1,0:T(8,128)(2,1)}, u32[]{:S(2)}, u32[]{:S(2)}) async-start(bf16[4,224,1024]{2,1,0:T(8,128)(2,1)} %bitcast.94), calls=%async_computation.5 | async-start | bytes 3670016 | tf_op jit(solution)/shard_map/all_to_all | solution.py:22
  260.4 27.8 %all-to-all-start.2 = ((bf16[4,224,1024]{2,1,0:T(8,128)(2,1)}), bf16[4,224,1024]{2,1,0:T(8,128)(2,1)}, u32[]{:S(2)}, u32[]{:S(2)}) async-start(bf16[4,224,1024]{2,1,0:T(8,128)(2,1)} %bitcast.96), calls=%async_computation.2 | async-start | bytes 3670016 | tf_op jit(solution)/shard_map/all_to_all | solution.py:22
Sparse Core Ops, SparseCore 0:
  10.1 86.2 all-gather.10
  99.2 77.1 all-gather.8
  179.2 76.1 all-gather.6
where the time goes:
time: 299 us; the launch traced here: 298 us
  waiting for transfers between devices  185 us (62%)
  starting transfers between devices  57.3 us (19%)
  matrix products  15.7 us (5%)
  local copies, waits for them, and re-layouts  14.8 us (5%)
  between operations  13.4 us (4%)
  other arithmetic  12.1 us (4%)
    all_gather x3, waiting for transfers between devices, on_device(): lax.all_gather(out_grads[seq_index], 'tensor', axis=1, tiled=True)  109 us
    all_to_all x3, waiting for transfers between devices, cross_rotate(): lax.all_to_all(scaled, 'tensor', split_axis=1, concat_axis=0, tiled=True)  27 us
    all_to_all x3, waiting for transfers between devices, cross_rotate(): lax.all_to_all(stacked.astype(jnp.bfloat16), 'tensor', split_axis=0, conc...  26.5 us
    all_to_all x3, starting transfers between devices, cross_rotate(): lax.all_to_all(stacked.astype(jnp.bfloat16), 'tensor', split_axis=0, conc...  25.4 us
    all_to_all x3, waiting for transfers between devices, sum_at_owner(): lax.all_to_all(pieces, axis, split_axis=0, concat_axis=0, tiled=True)  21.1 us
    all_to_all x3, starting transfers between devices, cross_rotate(): lax.all_to_all(scaled, 'tensor', split_axis=1, concat_axis=0, tiled=True)  18.7 us
    all_to_all x3, starting transfers between devices, sum_at_owner(): lax.all_to_all(pieces, axis, split_axis=0, concat_axis=0, tiled=True)  13.2 us
    dot_general x3, matrix products, on_device(): lax.dot_general(rotated, lax.all_gather(out_grads[seq_index], 'tensor', a...  11 us
  transfers between devices with their start and end apart: 12, of which 9 were waited for; matrix products, arithmetic and copies ran while one was open for 13% of the time, Pallas kernels for 0%

commit v1 on v0

v1 whole, which is shorter than its diff:
```python
import math

import jax
import jax.numpy as jnp
import numpy as np
from jax import lax
from jax.experimental import pallas as pl
from jax.experimental.pallas import tpu as pltpu
from jax.sharding import PartitionSpec as P


FF = 14336
FACTOR_A = 28
SEQS = 3
X, Z, C, Y = 4, 8, 2, 4
LANES = 128
MIXED = X * Z
SHARE = 80


def sylvester(order):
    result = np.ones((1, 1))
    for _ in range(order.bit_length() - 1):
        result = np.kron(result, np.array([[1.0, 1.0], [1.0, -1.0]]))
    return result


def paley_matrix():
    residues = set((number * number % 13 for number in range(1, 13)))
    core_table = np.zeros((14, 14))
    core_table[0, 1:] = 1.0
    core_table[1:, 0] = 1.0
    for row_index in range(13):
        for col_index in range(13):
            offset = (col_index - row_index) % 13
            if offset != 0:
                core_table[1 + row_index, 1 + col_index] = 1.0 if offset in residues else -1.0
    return np.kron(core_table, np.array([[1.0, 1.0], [1.0, -1.0]])) + np.kron(
        np.eye(14), np.array([[1.0, -1.0], [-1.0, -1.0]])
    )


def place(x, z, c):
    return (x % X) * Z * C + (z % Z) * C + c


def pairs_of(target):
    return [
        (place(x, z, c), place(*target(x, z, c)))
        for x in range(X)
        for z in range(Z)
        for c in range(C)
    ]


CORE_SWAP = pairs_of(lambda x, z, c: (x, z, 1 - c))
X_UP = pairs_of(lambda x, z, c: (x + 1, z, c))
X_DOWN = pairs_of(lambda x, z, c: (x - 1, z, c))
Z_UP = pairs_of(lambda x, z, c: (x, z + 1, c))
Z_DOWN = pairs_of(lambda x, z, c: (x, z - 1, c))
Z_UP2 = pairs_of(lambda x, z, c: (x, z + 2, c))
Z_DOWN2 = pairs_of(lambda x, z, c: (x, z - 2, c))
Y_UP = [(y, (y + 1) % Y) for y in range(Y)]
Y_DOWN = [(y, (y - 1) % Y) for y in range(Y)]
XY_SWAP = [
    (y * X * Z * C + place(x, z, c), x * X * Z * C + place(y, z, c))
    for y in range(Y)
    for x in range(X)
    for z in range(Z)
    for c in range(C)
]
XZ_GROUPS = [[place(x, z, c) for x in range(X) for z in range(Z)] for c in range(C)]
PARCELS = ((0, -1, 1), (-2, -3, 2, 3), (4,))
FAR_CUTS = (1, 2, 1)
VMEM = pl.BlockSpec(memory_space=pltpu.VMEM)
SMEM = pl.BlockSpec(memory_space=pltpu.SMEM)


def call(kernel, out_shape, in_specs, flops, limit_mib, scratch=()):
    many = isinstance(out_shape, tuple)
    return pl.pallas_call(
        kernel,
        out_shape=out_shape,
        in_specs=in_specs,
        out_specs=(VMEM,) * len(out_shape) if many else VMEM,
        scratch_shapes=list(scratch),
        cost_estimate=pl.CostEstimate(flops=flops, bytes_accessed=2**20, transcendentals=0),
        compiler_params=pltpu.CompilerParams(vmem_limit_bytes=limit_mib * 2**20),
    )


def chip_rotation_kernel(place_ref, acts_ref, got_ref, rot_ref, out_ref):
    core = place_ref[0]
    half = got_ref.shape[1]
    rows = 7 * half // 2
    start = pl.multiple_of(core * half, half)
    for s in range(SEQS):
        inner = jnp.dot(
            acts_ref[s, pl.ds(start, half), :], rot_ref[core], preferred_element_type=jnp.float32
        ) + jnp.dot(got_ref[s], rot_ref[1 - core], preferred_element_type=jnp.float32)
        inner = inner.astype(jnp.bfloat16)
        for j in range(3):
            out_ref[rows * s + half * j : rows * s + half * (j + 1), :] = inner[
                :, LANES * j : LANES * (j + 1)
            ]
        out_ref[rows * s + half * 3 : rows * (s + 1), :] = jnp.concatenate(
            [inner[: half // 2, 3 * LANES :], inner[half // 2 :, 3 * LANES :]], axis=1
        )
    out_ref[rows * SEQS :, :] = jnp.zeros((MIXED * SHARE - rows * SEQS, LANES), jnp.bfloat16)


def butterfly(values):
    values = list(values)
    step = 1
    while step < len(values):
        for low in range(len(values)):
            if not low & step:
                a, b = values[low], values[low | step]
                values[low], values[low | step] = a + b, a - b
        step *= 2
    return values


def mix_kernel(scale, in_ref, out_ref, mid_ref):
    for r in range(0, SHARE, 16):
        rows = slice(r, r + 16)
        for x in range(X):
            mixed = butterfly([in_ref[x * Z + z, rows, :].astype(jnp.float32) for z in range(Z)])
            for z in range(Z):
                mid_ref[x * Z + z] = mixed[z]
        for z in range(Z):
            mixed = butterfly([mid_ref[x * Z + z] for x in range(X)])
            for x in range(X):
                out_ref[x * Z + z, rows, :] = (mixed[x] * scale).astype(jnp.bfloat16)


def partial_kernel(place_ref, r0, r1, r2a, r2b, r3, *refs):
    refs, (own_ref, other_ref, lhs_ref) = list(refs[:-3]), refs[-3:]
    grads = []
    for parcel, cut in zip(PARCELS, FAR_CUTS):
        grads.append([refs.pop(0) for _ in range(5 if cut < len(parcel) else 4)] + [None])
        grads[-1] = grads[-1][:5]
    core, shift, z_index = place_ref[0], place_ref[1], place_ref[2]
    half = own_ref.shape[1]
    tok = lhs_ref.shape[2]
    rows = 7 * tok // 2
    cut = r2a.shape[0]

    def packed(d, start, count):
        if d != 2:
            return (r0, r1, None, r3)[d][start : start + count, :]
        if start + count <= cut:
            return r2a[start : start + count, :]
        if start >= cut:
            return r2b[start - cut : start - cut + count, :]
        return jnp.concatenate([r2a[start:, :], r2b[: start + count - cut, :]], axis=0)

    for d in range(Y):
        slot = lax.rem(d - shift + Y, Y)
        for s in range(SEQS):
            for j in range(3):
                lhs_ref[s, slot, :, LANES * j : LANES * (j + 1)] = packed(
                    d, rows * s + tok * j, tok
                )
            last = packed(d, rows * s + tok * 3, tok // 2)
            lhs_ref[s, slot, : tok // 2, 3 * LANES :] = last[:, : LANES // 2]
            lhs_ref[s, slot, tok // 2 :, 3 * LANES :] = last[:, LANES // 2 :]

    spots = [(p, i) for p, parcel in enumerate(PARCELS) for i in range(len(parcel))]

    def piece(k, at, s):
        p, i = spots[at]
        whole, after, before, far_first, far_last = grads[p]
        if k != 2:
            return (whole, after, None, before)[k][i, s]
        cut = FAR_CUTS[p]
        return far_first[i, s] if i < cut else far_last[i - cut, s]

    distances = [distance for parcel in PARCELS for distance in parcel]
    for s in range(SEQS):
        lhs = lhs_ref[s].reshape(Y * tok, 2 * half)
        for i in range(0, Z, 2):
            rhs = jnp.concatenate(
                [
                    jnp.concatenate([piece(k, i, s), piece(k, i + 1, s)], axis=1)
                    for k in range(X)
                ],
                axis=0,
            )
            both = lax.dot_general(
                lhs, rhs, (((0,), (0,)), ((), ())), preferred_element_type=jnp.float32
            )
            for at in range(2):
                column = lax.rem(z_index + distances[i + at] + Z, Z)
                columns = pl.ds(pl.multiple_of(column * LANES, LANES), LANES)
                low = both[:half, LANES * at : LANES * (at + 1)]
                high = both[half:, LANES * at : LANES * (at + 1)]
                own_ref[s, :, columns] = jnp.where(core == 0, low, high)
                other_ref[s, :, columns] = jnp.where(core == 0, high, low).astype(jnp.bfloat16)


def fisher_kernel(scale, own_ref, got_ref, out_ref):
    total = None
    for s in range(SEQS):
        value = own_ref[s] + got_ref[s].astype(jnp.float32)
        total = value * value if total is None else total + value * value
    out_ref[...] = total * scale


def exchange(array):
    return lax.all_to_all(
        array, "tensor", split_axis=0, concat_axis=0, tiled=True, axis_index_groups=XZ_GROUPS
    )


def on_device(hidden_acts, out_grads):
    seq_count, tok_rows, local_ff = hidden_acts.shape
    half = tok_rows // C
    width = C * local_ff
    features = Z * C * out_grads.shape[2]
    tensor_index = lax.axis_index("tensor")
    core = tensor_index % C
    z_index = tensor_index // C % Z
    x_index = tensor_index // (Z * C)
    y_index = lax.axis_index("dp")
    places = jnp.stack([core, (x_index - y_index + Y) % Y, z_index]).astype(jnp.int32)
    first = core == 0

    low, high = out_grads[:, :half], out_grads[:, half:]
    mine, other = jnp.where(first, low, high), jnp.where(first, high, low)
    got = lax.ppermute(other, "tensor", CORE_SWAP)
    piece = jnp.concatenate([jnp.where(first, mine, got), jnp.where(first, got, mine)], axis=2)
    piece = lax.ppermute(piece, ("dp", "tensor"), XY_SWAP)

    other = lax.dynamic_slice_in_dim(hidden_acts, (1 - core) * half, half, axis=1)
    got = lax.ppermute(other, "tensor", CORE_SWAP)
    local_rot = np.kron(sylvester(local_ff // FACTOR_A), paley_matrix())
    chip_rot = np.stack([np.hstack([local_rot, local_rot]), np.hstack([local_rot, -local_rot])])
    inner = call(
        chip_rotation_kernel,
        jax.ShapeDtypeStruct((MIXED * SHARE, LANES), jnp.bfloat16),
        [SMEM, VMEM, VMEM, VMEM],
        2 * seq_count * half * width * width,
        16,
    )(places, hidden_acts, got, jnp.asarray(chip_rot, jnp.bfloat16))
    inner = exchange(inner.reshape(MIXED, SHARE, LANES))
    mixed = call(
        lambda *refs: mix_kernel(1.0 / math.sqrt(FF), *refs),
        jax.ShapeDtypeStruct((MIXED, SHARE, LANES), jnp.bfloat16),
        [VMEM],
        10**8,
        16,
        [pltpu.VMEM((MIXED, 16, LANES), jnp.float32)],
    )(inner)
    rotated = exchange(mixed).reshape(MIXED * SHARE, LANES)

    below = lax.ppermute(rotated, "dp", Y_UP)
    above = lax.ppermute(rotated, "dp", Y_DOWN)
    cut = MIXED * SHARE // 2
    far_low = lax.ppermute(below[:cut], "dp", Y_UP)
    far_high = lax.ppermute(above[cut:], "dp", Y_DOWN)

    down1 = lax.ppermute(piece, "tensor", Z_UP)
    up1 = lax.ppermute(piece, "tensor", Z_DOWN)
    down23 = lax.ppermute(jnp.stack([piece, down1]), "tensor", Z_UP2)
    up23 = lax.ppermute(jnp.stack([piece, up1]), "tensor", Z_DOWN2)
    down4 = lax.ppermute(down23[1:], "tensor", Z_UP)

    grads = []

    def along_x(block, cut):
        before = lax.ppermute(block, "tensor", X_UP)
        after = lax.ppermute(block, "tensor", X_DOWN)
        grads.extend([block, after, before])
        grads.append(lax.ppermute(before[:cut], "tensor", X_UP))
        if cut < block.shape[0]:
            grads.append(lax.ppermute(after[cut:], "tensor", X_DOWN))

    along_x(jnp.stack([piece, down1, up1]), FAR_CUTS[0])
    along_x(jnp.concatenate([down23, up23]), FAR_CUTS[1])
    along_x(down4, FAR_CUTS[2])
    own, sent = call(
        partial_kernel,
        (
            jax.ShapeDtypeStruct((seq_count, local_ff, features), jnp.float32),
            jax.ShapeDtypeStruct((seq_count, local_ff, features), jnp.bfloat16),
        ),
        [SMEM] + [VMEM] * (5 + len(grads)),
        2 * seq_count * half * Y * width * features,
        40,
        [pltpu.VMEM((seq_count, Y, half, width), jnp.bfloat16)],
    )(places, rotated, above, far_low, far_high, below, *grads)
    got = lax.ppermute(sent, "tensor", CORE_SWAP)
    return call(
        lambda *refs: fisher_kernel(1.0 / (tok_rows * Y * SEQS), *refs),
        jax.ShapeDtypeStruct((local_ff, features), jnp.float32),
        [VMEM, VMEM],
        10**7,
        16,
    )(own, got)


def solution(mesh):
    placed = (P(None, "dp", "tensor"), P(None, "dp", "tensor"))

    return jax.shard_map(
        on_device, mesh=mesh, in_specs=placed, out_specs=P("tensor", "dp"), check_vma=False
    )
```

time: 299 us -> 147 us (0.49)
  waiting for transfers between devices: 185 us -> 60 us
  matrix products: 15.7 us -> 0 us
  between operations: 13.4 us -> 0.18 us
  starting transfers between devices: 57.3 us -> 70.3 us
  other arithmetic: 12.1 us -> 0.37 us
  Pallas kernels: 0 us -> 9.99 us
  local copies, waits for them, and re-layouts: 14.8 us -> 6.11 us
    all_gather x3 -> x0, waiting for transfers between devices: 109 us -> none  [on_device(): lax.all_gather(out_grads[seq_index], 'tensor', axis=1, tiled=True)]
    all_to_all x9 -> x2, waiting for transfers between devices: 74.6 us -> 14.6 us  [exchange(): lax.all_to_all(array, 'tensor', split_axis=0, concat_axis=0, tiled=True,...]
    ppermute x0 -> x24, starting transfers between devices: none -> 52.8 us  [the longest x3 21.2 us: along_x(): after = lax.ppermute(block, 'tensor', X_DOWN)]
    ppermute x0 -> x24, waiting for transfers between devices: none -> 45.4 us  [the longest x1 16 us: on_device(): up1 = lax.ppermute(piece, 'tensor', Z_DOWN)]
    all_to_all x9 -> x2, starting transfers between devices: 57.2 us -> 17.4 us  [exchange(): lax.all_to_all(array, 'tensor', split_axis=0, concat_axis=0, tiled=True,...]
    dot_general x9 -> x0, matrix products: 15.7 us -> none  [the longest x3 11 us: on_device(): lax.dot_general(rotated, lax.all_gather(out_grads[seq_index], 'tensor', a...]
    pallas_call x0 -> x4, Pallas kernels: none -> 9.99 us  [the longest x1 5.49 us: on_device(): call(partial_kernel, (jax.ShapeDtypeStruct((seq_count, local_ff, features...]
    reshape x6 -> x0, local copies, waits for them, and re-layouts: 4.77 us -> none  [the longest x3 4.38 us: cut_along(): array.reshape(*shape[:dim], count, shape[dim] // count, *shape[dim + 1:])]
  transfers between devices with their start and end apart: 12 -> 26, of which waited for: 9 -> 15; matrix products, arithmetic and copies ran while one was open for 13% -> 2% of each run, Pallas kernels for 0% -> 0%
where the time goes in v1:
time: 147 us
  starting transfers between devices  70.3 us (48%)
  waiting for transfers between devices  60 us (41%)
  Pallas kernels  9.99 us (7%)
  local copies, waits for them, and re-layouts  6.11 us (4%)
    ppermute x3, starting transfers between devices, along_x(): after = lax.ppermute(block, 'tensor', X_DOWN)  21.2 us
    all_to_all x2, starting transfers between devices, exchange(): lax.all_to_all(array, 'tensor', split_axis=0, concat_axis=0, tiled=True,...  17.4 us
    ppermute x1, waiting for transfers between devices, on_device(): up1 = lax.ppermute(piece, 'tensor', Z_DOWN)  16 us
    all_to_all x2, waiting for transfers between devices, exchange(): lax.all_to_all(array, 'tensor', split_axis=0, concat_axis=0, tiled=True,...  14.6 us
    ppermute x3, waiting for transfers between devices, along_x(): before = lax.ppermute(block, 'tensor', X_UP)  7.96 us
    ppermute x1, waiting for transfers between devices, on_device(): down4 = lax.ppermute(down23[1:], 'tensor', Z_UP)  5.75 us
    pallas_call x1, Pallas kernels, on_device(): call(partial_kernel, (jax.ShapeDtypeStruct((seq_count, local_ff, features...  5.49 us
    ppermute x1, starting transfers between devices, on_device(): got = lax.ppermute(sent, 'tensor', CORE_SWAP)  5.2 us
  transfers between devices with their start and end apart: 26, of which 15 were waited for; matrix products, arithmetic and copies ran while one was open for 2% of the time, Pallas kernels for 0%

profile of v1, /device:TPU:1, one launch (start us, length us, event | category | flops | bytes accessed | tf_op | source)
XLA Modules:
  0.0 147.0 jit_solution(7845254922455826413)
XLA Ops:
  1.0 3.3 %collective-permute-start = (bf16[3,224,224]{2,1,0:T(8,128)(2,1)S(1)}, bf16[3,224,224]{2,1,0:T(8,128)(2,1)S(1)}, u32[]{:S(2)}, u32[]{:S(2)}) collective-permute-start(bf16[3,224,224]{2,1,0:T(8,128)(2,1)S(1)} %constant_dynamic-slice_fusion), channel_id=1, source_target_pairs={{0,1},{1,0},{2,3},{3,2},{4,5},{5,4},{6,7},{7,6},{8,9},{9,8},{10,11... | collective-permute-start | bytes 903176 | tf_op jit(solution)/shard_map/ppermute | solution.py:236
  7.7 2.0 %shard_map.37 = bf16[2560,128]{1,0:T(8,128)(2,1)} custom-call(s32[3]{0:T(128)S(1)} %pad_add_fusion.place_ref, bf16[3,448,224]{2,1,0:T(8,128)(2,1)S(1)} %copy-done, bf16[3,224,224]{2,1,0:T(8,128)(2,1)S(1)} %collective-permute-done.got_ref, bf16[2,224,448]{2,1,0:T(8,128)(2,1)S(1)} %copy-done.1), custom_call_target="tpu_custom_call" | custom-call | flops 269746176 | bytes 1048576 | tf_op jit(solution)/shard_map/pallas_call | solution.py:239
  9.7 9.3 %all-to-all-start = ((bf16[32,80,128]{2,1,0:T(8,128)(2,1)}), bf16[32,80,128]{2,1,0:T(8,128)(2,1)S(1)}, u32[]{:S(2)}, u32[]{:S(2)}) async-start(bf16[32,80,128]{2,1,0:T(8,128)(2,1)} %bitcast.3), calls=%async_computation | async-start | bytes 1310720 | tf_op jit(solution)/shard_map/all_to_all | solution.py:211
  21.3 14.6 %all-to-all-done.refs_0_ = bf16[32,80,128]{2,1,0:T(8,128)(2,1)S(1)} async-done(((bf16[32,80,128]{2,1,0:T(8,128)(2,1)}), bf16[32,80,128]{2,1,0:T(8,128)(2,1)S(1)}, u32[]{:S(2)}, u32[]{:S(2)}) %all-to-all-start) | async-done | bytes 655392 | tf_op jit(solution)/shard_map/all_to_all | solution.py:211
  35.9 1.2 shard_map.38
  37.1 8.1 %all-to-all-start.1 = ((bf16[32,80,128]{2,1,0:T(8,128)(2,1)}), bf16[32,80,128]{2,1,0:T(8,128)(2,1)S(1)}, u32[]{:S(2)}, u32[]{:S(2)}) async-start(bf16[32,80,128]{2,1,0:T(8,128)(2,1)} %shard_map.38), calls=%async_computation.1 | async-start | bytes 1310720 | tf_op jit(solution)/shard_map/all_to_all | solution.py:211
  46.0 2.5 %collective-permute-start.8 = (bf16[3,224,128]{2,1,0:T(8,128)(2,1)S(1)}, bf16[3,224,128]{2,1,0:T(8,128)(2,1)S(1)}, u32[]{:S(2)}, u32[]{:S(2)}) collective-permute-start(bf16[3,224,128]{2,1,0:T(8,128)(2,1)S(1)} %collective-permute-done.6), channel_id=1, source_target_pairs={{0,14},{1,15},{2,0},{3,1},{4,2},{5,3},{6,4},{7,5},{8,6},{9,7},{10,... | collective-permute-start | bytes 516104 | tf_op jit(solution)/shard_map/ppermute | solution.py:264
  48.5 16.0 %collective-permute-done.8 = bf16[3,224,128]{2,1,0:T(8,128)(2,1)S(1)} collective-permute-done((bf16[3,224,128]{2,1,0:T(8,128)(2,1)S(1)}, bf16[3,224,128]{2,1,0:T(8,128)(2,1)S(1)}, u32[]{:S(2)}, u32[]{:S(2)}) %collective-permute-start.8) | collective-permute-done | bytes 172064 | tf_op jit(solution)/shard_map/ppermute | solution.py:264
  66.0 3.3 %collective-permute-start.14 = (bf16[2,3,224,128]{3,2,1,0:T(8,128)(2,1)S(1)}, bf16[2,3,224,128]{3,2,1,0:T(8,128)(2,1)S(1)}, u32[]{:S(2)}, u32[]{:S(2)}) collective-permute-start(bf16[2,3,224,128]{3,2,1,0:T(8,128)(2,1)S(1)} %get-tuple-element.13), channel_id=1, source_target_pairs={{0,12},{1,13},{2,14},{3,15},{4,0},{5,1},{6,2},{7,3},{8,4},{9,5},{1... | collective-permute-start | bytes 1032200 | tf_op jit(solution)/shard_map/ppermute | solution.py:266
  70.1 10.0 %collective-permute-start.9 = (bf16[3,3,224,128]{3,2,1,0:T(8,128)(2,1)S(1)}, bf16[3,3,224,128]{3,2,1,0:T(8,128)(2,1)S(1)}, u32[]{:S(2)}, u32[]{:S(2)}) collective-permute-start(bf16[3,3,224,128]{3,2,1,0:T(8,128)(2,1)S(1)} %pad_maximum_fusion.refs_0_), channel_id=1, source_target_pairs={{0,48},{1,49},{2,50},{3,51},{4,52},{5,53},{6,54},{7,55},{8,56},{9,... | collective-permute-start | bytes 1548296 | tf_op jit(solution)/shard_map/ppermute | solution.py:273
  80.2 3.1 %collective-permute-done.13 = bf16[2,3,224,128]{3,2,1,0:T(8,128)(2,1)S(1)} collective-permute-done((bf16[2,3,224,128]{3,2,1,0:T(8,128)(2,1)S(1)}, bf16[2,3,224,128]{3,2,1,0:T(8,128)(2,1)S(1)}, u32[]{:S(2)}, u32[]{:S(2)}) %collective-permute-start.13) | collective-permute-done | bytes 344096 | tf_op jit(solution)/shard_map/ppermute | solution.py:265
  85.1 10.0 %collective-permute-start.15 = (bf16[4,3,224,128]{3,2,1,0:T(8,128)(2,1)}, bf16[4,3,224,128]{3,2,1,0:T(8,128)(2,1)S(1)}, u32[]{:S(2)}, u32[]{:S(2)}) collective-permute-start(bf16[4,3,224,128]{3,2,1,0:T(8,128)(2,1)} %constant_dynamic-update-slice_fusion.refs_5_), channel_id=1, source_target_pairs={{0,48},{1,49},{2,50},{3,51},{4,52},{5,53},{6,54},{7,55},{8,56},{9,... | collective-permute-start | bytes 2064392 | tf_op jit(solution)/shard_map/ppermute | solution.py:273
  95.2 5.7 %collective-permute-done.19.refs_10_ = bf16[1,3,224,128]{3,2,1,0:T(8,128)(2,1)S(1)} collective-permute-done((bf16[1,3,224,128]{3,2,1,0:T(8,128)(2,1)S(1)}, bf16[1,3,224,128]{3,2,1,0:T(8,128)(2,1)S(1)}, u32[]{:S(2)}, u32[]{:S(2)}) %collective-permute-start.19) | collective-permute-done | bytes 172064 | tf_op jit(solution)/shard_map/ppermute | solution.py:267
  100.9 4.2 %collective-permute-start.1 = (bf16[2560,128]{1,0:T(8,128)(2,1)S(1)}, bf16[2560,128]{1,0:T(8,128)(2,1)S(1)}, u32[]{:S(2)}, u32[]{:S(2)}) collective-permute-start(bf16[2560,128]{1,0:T(8,128)(2,1)S(1)} %bitcast.9), channel_id=1, source_target_pairs={{0,192},{64,0},{128,64},{192,128},{1,193},{65,1},{129,65},{193,129... | collective-permute-start | bytes 1966088 | tf_op jit(solution)/shard_map/ppermute | solution.py:258
  105.1 8.0 %collective-permute-done.21.refs_12_ = bf16[1,3,224,128]{3,2,1,0:T(8,128)(2,1)S(1)} collective-permute-done((bf16[1,3,224,128]{3,2,1,0:T(8,128)(2,1)S(1)}, bf16[1,3,224,128]{3,2,1,0:T(8,128)(2,1)S(1)}, u32[]{:S(2)}, u32[]{:S(2)}) %collective-permute-start.21) | collective-permute-done | bytes 172064 | tf_op jit(solution)/shard_map/ppermute | solution.py:272
  115.8 1.9 %collective-permute-done.20.refs_11_ = bf16[1,3,224,128]{3,2,1,0:T(8,128)(2,1)S(1)} collective-permute-done((bf16[1,3,224,128]{3,2,1,0:T(8,128)(2,1)S(1)}, bf16[1,3,224,128]{3,2,1,0:T(8,128)(2,1)S(1)}, u32[]{:S(2)}, u32[]{:S(2)}) %collective-permute-start.20) | collective-permute-done | bytes 172064 | tf_op jit(solution)/shard_map/ppermute | solution.py:273
  117.6 2.4 %collective-permute-start.12 = (bf16[2,3,224,128]{3,2,1,0:T(8,128)(2,1)S(1)}, bf16[2,3,224,128]{3,2,1,0:T(8,128)(2,1)S(1)}, u32[]{:S(2)}, u32[]{:S(2)}) collective-permute-start(bf16[2,3,224,128]{3,2,1,0:T(8,128)(2,1)S(1)} %slice.39), channel_id=1, source_target_pairs={{0,48},{1,49},{2,50},{3,51},{4,52},{5,53},{6,54},{7,55},{8,56},{9,... | collective-permute-start | bytes 1032200 | tf_op jit(solution)/shard_map/ppermute | solution.py:277
  120.0 2.7 %collective-permute-start.18 = (bf16[2,3,224,128]{3,2,1,0:T(8,128)(2,1)S(1)}, bf16[2,3,224,128]{3,2,1,0:T(8,128)(2,1)S(1)}, u32[]{:S(2)}, u32[]{:S(2)}) collective-permute-start(bf16[2,3,224,128]{3,2,1,0:T(8,128)(2,1)S(1)} %slice.41), channel_id=1, source_target_pairs={{0,48},{1,49},{2,50},{3,51},{4,52},{5,53},{6,54},{7,55},{8,56},{9,... | collective-permute-start | bytes 1032200 | tf_op jit(solution)/shard_map/ppermute | solution.py:277
  123.3 4.9 %collective-permute-start.4 = (bf16[1280,128]{1,0:T(8,128)(2,1)S(1)}, bf16[1280,128]{1,0:T(8,128)(2,1)S(1)}, u32[]{:S(2)}, u32[]{:S(2)}) collective-permute-start(bf16[1280,128]{1,0:T(8,128)(2,1)S(1)} %slice.37), channel_id=1, source_target_pairs={{0,192},{64,0},{128,64},{192,128},{1,193},{65,1},{129,65},{193,129... | collective-permute-start | bytes 983048 | tf_op jit(solution)/shard_map/ppermute | solution.py:261
  128.2 3.2 %collective-permute-done.17.refs_8_ = bf16[2,3,224,128]{3,2,1,0:T(8,128)(2,1)S(1)} collective-permute-done((bf16[2,3,224,128]{3,2,1,0:T(8,128)(2,1)S(1)}, bf16[2,3,224,128]{3,2,1,0:T(8,128)(2,1)S(1)}, u32[]{:S(2)}, u32[]{:S(2)}) %collective-permute-start.17) | collective-permute-done | bytes 344096 | tf_op jit(solution)/shard_map/ppermute | solution.py:275
  132.2 5.5 %shard_map.39 = (f32[3,224,1024]{2,1,0:T(8,128)S(1)}, bf16[3,224,1024]{2,1,0:T(8,128)(2,1)S(1)}) custom-call(s32[3]{0:T(128)S(1)} %pad_add_fusion.place_ref, bf16[2560,128]{1,0:T(8,128)(2,1)S(1)} %bitcast.10, bf16[2560,128]{1,0:T(8,128)(2,1)S(1)} %collective-permute-done.1.r1, bf16[1280,128]{1,0:T(8,128)(2,1)S(1)} %collective-permute-done.3.r2a, ...), custom_call_target="tpu_custom_call" | custom-call | flops 2466250752 | bytes 1048576 | tf_op jit(solution)/shard_map/pallas_call | solution.py:282
  137.7 5.2 %collective-permute-start.23 = (bf16[3,224,1024]{2,1,0:T(8,128)(2,1)S(1)}, bf16[3,224,1024]{2,1,0:T(8,128)(2,1)S(1)}, u32[]{:S(2)}, u32[]{:S(2)}) collective-permute-start(bf16[3,224,1024]{2,1,0:T(8,128)(2,1)S(1)} %get-tuple-element.8), channel_id=1, source_target_pairs={{0,1},{1,0},{2,3},{3,2},{4,5},{5,4},{6,7},{7,6},{8,9},{9,8},{10,11... | collective-permute-start | bytes 4128776 | tf_op jit(solution)/shard_map/ppermute | solution.py:293
  142.9 2.8 %collective-permute-done.23.refs_1_ = bf16[3,224,1024]{2,1,0:T(8,128)(2,1)S(1)} collective-permute-done((bf16[3,224,1024]{2,1,0:T(8,128)(2,1)S(1)}, bf16[3,224,1024]{2,1,0:T(8,128)(2,1)S(1)}, u32[]{:S(2)}, u32[]{:S(2)}) %collective-permute-start.23) | collective-permute-done | bytes 1376288 | tf_op jit(solution)/shard_map/ppermute | solution.py:293
  145.6 1.3 shard_map.40
  (57 shorter events, 15.7 us)
Async XLA Ops:
  1.0 4.6 %collective-permute-start = (bf16[3,224,224]{2,1,0:T(8,128)(2,1)S(1)}, bf16[3,224,224]{2,1,0:T(8,128)(2,1)S(1)}, u32[]{:S(2)}, u32[]{:S(2)}) collective-permute-start(bf16[3,224,224]{2,1,0:T(8,128)(2,1)S(1)} %constant_dynamic-slice_fusion), channel_id=1, source_target_pairs={{0,1},{1,0},{2,3},{3,2},{4,5},{5,4},{6,7},{7,6},{8,9},{9,8},{10,11... | collective-permute-start | bytes 903176 | tf_op jit(solution)/shard_map/ppermute | solution.py:236
  9.7 26.2 %all-to-all-start = ((bf16[32,80,128]{2,1,0:T(8,128)(2,1)}), bf16[32,80,128]{2,1,0:T(8,128)(2,1)S(1)}, u32[]{:S(2)}, u32[]{:S(2)}) async-start(bf16[32,80,128]{2,1,0:T(8,128)(2,1)} %bitcast.3), calls=%async_computation | async-start | bytes 1310720 | tf_op jit(solution)/shard_map/all_to_all | solution.py:211
  37.1 63.8 %all-to-all-start.1 = ((bf16[32,80,128]{2,1,0:T(8,128)(2,1)}), bf16[32,80,128]{2,1,0:T(8,128)(2,1)S(1)}, u32[]{:S(2)}, u32[]{:S(2)}) async-start(bf16[32,80,128]{2,1,0:T(8,128)(2,1)} %shard_map.38), calls=%async_computation.1 | async-start | bytes 1310720 | tf_op jit(solution)/shard_map/all_to_all | solution.py:211
  46.0 18.5 %collective-permute-start.8 = (bf16[3,224,128]{2,1,0:T(8,128)(2,1)S(1)}, bf16[3,224,128]{2,1,0:T(8,128)(2,1)S(1)}, u32[]{:S(2)}, u32[]{:S(2)}) collective-permute-start(bf16[3,224,128]{2,1,0:T(8,128)(2,1)S(1)} %collective-permute-done.6), channel_id=1, source_target_pairs={{0,14},{1,15},{2,0},{3,1},{4,2},{5,3},{6,4},{7,5},{8,6},{9,7},{10,... | collective-permute-start | bytes 516104 | tf_op jit(solution)/shard_map/ppermute | solution.py:264
  48.5 17.1 %collective-permute-start.7 = (bf16[3,224,128]{2,1,0:T(8,128)(2,1)S(1)}, bf16[3,224,128]{2,1,0:T(8,128)(2,1)S(1)}, u32[]{:S(2)}, u32[]{:S(2)}) collective-permute-start(bf16[3,224,128]{2,1,0:T(8,128)(2,1)S(1)} %collective-permute-done.6), channel_id=1, source_target_pairs={{0,2},{1,3},{2,4},{3,5},{4,6},{5,7},{6,8},{7,9},{8,10},{9,11},{10,... | collective-permute-start | bytes 516104 | tf_op jit(solution)/shard_map/ppermute | solution.py:263
  65.6 17.6 %collective-permute-start.13 = (bf16[2,3,224,128]{3,2,1,0:T(8,128)(2,1)S(1)}, bf16[2,3,224,128]{3,2,1,0:T(8,128)(2,1)S(1)}, u32[]{:S(2)}, u32[]{:S(2)}) collective-permute-start(bf16[2,3,224,128]{3,2,1,0:T(8,128)(2,1)S(1)} %get-tuple-element.14), channel_id=1, source_target_pairs={{0,4},{1,5},{2,6},{3,7},{4,8},{5,9},{6,10},{7,11},{8,12},{9,13},{1... | collective-permute-start | bytes 1032200 | tf_op jit(solution)/shard_map/ppermute | solution.py:265
  66.0 18.3 %collective-permute-start.14 = (bf16[2,3,224,128]{3,2,1,0:T(8,128)(2,1)S(1)}, bf16[2,3,224,128]{3,2,1,0:T(8,128)(2,1)S(1)}, u32[]{:S(2)}, u32[]{:S(2)}) collective-permute-start(bf16[2,3,224,128]{3,2,1,0:T(8,128)(2,1)S(1)} %get-tuple-element.13), channel_id=1, source_target_pairs={{0,12},{1,13},{2,14},{3,15},{4,0},{5,1},{6,2},{7,3},{8,4},{9,5},{1... | collective-permute-start | bytes 1032200 | tf_op jit(solution)/shard_map/ppermute | solution.py:266
  69.4 31.6 %collective-permute-start.10 = (bf16[3,3,224,128]{3,2,1,0:T(8,128)(2,1)S(1)}, bf16[3,3,224,128]{3,2,1,0:T(8,128)(2,1)}, u32[]{:S(2)}, u32[]{:S(2)}) collective-permute-start(bf16[3,3,224,128]{3,2,1,0:T(8,128)(2,1)S(1)} %pad_maximum_fusion.refs_0_), channel_id=1, source_target_pairs={{0,16},{1,17},{2,18},{3,19},{4,20},{5,21},{6,22},{7,23},{8,24},{9,... | collective-permute-start | bytes 1548296 | tf_op jit(solution)/shard_map/ppermute | solution.py:272
  70.1 35.0 %collective-permute-start.9 = (bf16[3,3,224,128]{3,2,1,0:T(8,128)(2,1)S(1)}, bf16[3,3,224,128]{3,2,1,0:T(8,128)(2,1)S(1)}, u32[]{:S(2)}, u32[]{:S(2)}) collective-permute-start(bf16[3,3,224,128]{3,2,1,0:T(8,128)(2,1)S(1)} %pad_maximum_fusion.refs_0_), channel_id=1, source_target_pairs={{0,48},{1,49},{2,50},{3,51},{4,52},{5,53},{6,54},{7,55},{8,56},{9,... | collective-permute-start | bytes 1548296 | tf_op jit(solution)/shard_map/ppermute | solution.py:273
  85.1 30.1 %collective-permute-start.16 = (bf16[4,3,224,128]{3,2,1,0:T(8,128)(2,1)}, bf16[4,3,224,128]{3,2,1,0:T(8,128)(2,1)S(1)}, u32[]{:S(2)}, u32[]{:S(2)}) collective-permute-start(bf16[4,3,224,128]{3,2,1,0:T(8,128)(2,1)} %constant_dynamic-update-slice_fusion.refs_5_), channel_id=1, source_target_pairs={{0,16},{1,17},{2,18},{3,19},{4,20},{5,21},{6,22},{7,23},{8,24},{9,... | collective-permute-start | bytes 2064392 | tf_op jit(solution)/shard_map/ppermute | solution.py:272
  85.1 30.5 %collective-permute-start.15 = (bf16[4,3,224,128]{3,2,1,0:T(8,128)(2,1)}, bf16[4,3,224,128]{3,2,1,0:T(8,128)(2,1)S(1)}, u32[]{:S(2)}, u32[]{:S(2)}) collective-permute-start(bf16[4,3,224,128]{3,2,1,0:T(8,128)(2,1)} %constant_dynamic-update-slice_fusion.refs_5_), channel_id=1, source_target_pairs={{0,48},{1,49},{2,50},{3,51},{4,52},{5,53},{6,54},{7,55},{8,56},{9,... | collective-permute-start | bytes 2064392 | tf_op jit(solution)/shard_map/ppermute | solution.py:273
  95.1 5.8 %collective-permute-start.19 = (bf16[1,3,224,128]{3,2,1,0:T(8,128)(2,1)S(1)}, bf16[1,3,224,128]{3,2,1,0:T(8,128)(2,1)S(1)}, u32[]{:S(2)}, u32[]{:S(2)}) collective-permute-start(bf16[1,3,224,128]{3,2,1,0:T(8,128)(2,1)S(1)} %slice.42), channel_id=1, source_target_pairs={{0,2},{1,3},{2,4},{3,5},{4,6},{5,7},{6,8},{7,9},{8,10},{9,11},{10,... | collective-permute-start | bytes 516104 | tf_op jit(solution)/shard_map/ppermute | solution.py:267
  100.9 19.1 %collective-permute-start.2 = (bf16[2560,128]{1,0:T(8,128)(2,1)S(1)}, bf16[2560,128]{1,0:T(8,128)(2,1)S(1)}, u32[]{:S(2)}, u32[]{:S(2)}) collective-permute-start(bf16[2560,128]{1,0:T(8,128)(2,1)S(1)} %bitcast.8), channel_id=1, source_target_pairs={{0,64},{64,128},{128,192},{192,0},{1,65},{65,129},{129,193},{193,1... | collective-permute-start | bytes 1966088 | tf_op jit(solution)/shard_map/ppermute | solution.py:257
  100.9 19.1 %collective-permute-start.1 = (bf16[2560,128]{1,0:T(8,128)(2,1)S(1)}, bf16[2560,128]{1,0:T(8,128)(2,1)S(1)}, u32[]{:S(2)}, u32[]{:S(2)}) collective-permute-start(bf16[2560,128]{1,0:T(8,128)(2,1)S(1)} %bitcast.9), channel_id=1, source_target_pairs={{0,192},{64,0},{128,64},{192,128},{1,193},{65,1},{129,65},{193,129... | collective-permute-start | bytes 1966088 | tf_op jit(solution)/shard_map/ppermute | solution.py:258
  105.1 8.0 %collective-permute-start.21 = (bf16[1,3,224,128]{3,2,1,0:T(8,128)(2,1)S(1)}, bf16[1,3,224,128]{3,2,1,0:T(8,128)(2,1)S(1)}, u32[]{:S(2)}, u32[]{:S(2)}) collective-permute-start(bf16[1,3,224,128]{3,2,1,0:T(8,128)(2,1)S(1)} %collective-permute-done.19.refs_10_), channel_id=1, source_target_pairs={{0,16},{1,17},{2,18},{3,19},{4,20},{5,21},{6,22},{7,23},{8,24},{9,... | collective-permute-start | bytes 516104 | tf_op jit(solution)/shard_map/ppermute | solution.py:272
  113.1 4.6 %collective-permute-start.20 = (bf16[1,3,224,128]{3,2,1,0:T(8,128)(2,1)S(1)}, bf16[1,3,224,128]{3,2,1,0:T(8,128)(2,1)S(1)}, u32[]{:S(2)}, u32[]{:S(2)}) collective-permute-start(bf16[1,3,224,128]{3,2,1,0:T(8,128)(2,1)S(1)} %collective-permute-done.19.refs_10_), channel_id=1, source_target_pairs={{0,48},{1,49},{2,50},{3,51},{4,52},{5,53},{6,54},{7,55},{8,56},{9,... | collective-permute-start | bytes 516104 | tf_op jit(solution)/shard_map/ppermute | solution.py:273
  115.2 7.6 %collective-permute-start.11 = (bf16[1,3,224,128]{3,2,1,0:T(8,128)(2,1)S(1)}, bf16[1,3,224,128]{3,2,1,0:T(8,128)(2,1)S(1)}, u32[]{:S(2)}, u32[]{:S(2)}) collective-permute-start(bf16[1,3,224,128]{3,2,1,0:T(8,128)(2,1)S(1)} %slice.38), channel_id=1, source_target_pairs={{0,16},{1,17},{2,18},{3,19},{4,20},{5,21},{6,22},{7,23},{8,24},{9,... | collective-permute-start | bytes 516104 | tf_op jit(solution)/shard_map/ppermute | solution.py:275
  115.6 7.7 %collective-permute-start.22 = (bf16[1,3,224,128]{3,2,1,0:T(8,128)(2,1)S(1)}, bf16[1,3,224,128]{3,2,1,0:T(8,128)(2,1)S(1)}, u32[]{:S(2)}, u32[]{:S(2)}) collective-permute-start(bf16[1,3,224,128]{3,2,1,0:T(8,128)(2,1)S(1)} %collective-permute-done.21.refs_12_), channel_id=1, source_target_pairs={{0,16},{1,17},{2,18},{3,19},{4,20},{5,21},{6,22},{7,23},{8,24},{9,... | collective-permute-start | bytes 516104 | tf_op jit(solution)/shard_map/ppermute | solution.py:275
  117.6 10.5 %collective-permute-start.12 = (bf16[2,3,224,128]{3,2,1,0:T(8,128)(2,1)S(1)}, bf16[2,3,224,128]{3,2,1,0:T(8,128)(2,1)S(1)}, u32[]{:S(2)}, u32[]{:S(2)}) collective-permute-start(bf16[2,3,224,128]{3,2,1,0:T(8,128)(2,1)S(1)} %slice.39), channel_id=1, source_target_pairs={{0,48},{1,49},{2,50},{3,51},{4,52},{5,53},{6,54},{7,55},{8,56},{9,... | collective-permute-start | bytes 1032200 | tf_op jit(solution)/shard_map/ppermute | solution.py:277
  120.0 11.3 %collective-permute-start.17 = (bf16[2,3,224,128]{3,2,1,0:T(8,128)(2,1)S(1)}, bf16[2,3,224,128]{3,2,1,0:T(8,128)(2,1)S(1)}, u32[]{:S(2)}, u32[]{:S(2)}) collective-permute-start(bf16[2,3,224,128]{3,2,1,0:T(8,128)(2,1)S(1)} %slice.40), channel_id=1, source_target_pairs={{0,16},{1,17},{2,18},{3,19},{4,20},{5,21},{6,22},{7,23},{8,24},{9,... | collective-permute-start | bytes 1032200 | tf_op jit(solution)/shard_map/ppermute | solution.py:275
  120.0 11.5 %collective-permute-start.18 = (bf16[2,3,224,128]{3,2,1,0:T(8,128)(2,1)S(1)}, bf16[2,3,224,128]{3,2,1,0:T(8,128)(2,1)S(1)}, u32[]{:S(2)}, u32[]{:S(2)}) collective-permute-start(bf16[2,3,224,128]{3,2,1,0:T(8,128)(2,1)S(1)} %slice.41), channel_id=1, source_target_pairs={{0,48},{1,49},{2,50},{3,51},{4,52},{5,53},{6,54},{7,55},{8,56},{9,... | collective-permute-start | bytes 1032200 | tf_op jit(solution)/shard_map/ppermute | solution.py:277
  122.8 8.8 %collective-permute-start.3 = (bf16[1280,128]{1,0:T(8,128)(2,1)S(1)}, bf16[1280,128]{1,0:T(8,128)(2,1)S(1)}, u32[]{:S(2)}, u32[]{:S(2)}) collective-permute-start(bf16[1280,128]{1,0:T(8,128)(2,1)S(1)} %slice.36), channel_id=1, source_target_pairs={{0,64},{64,128},{128,192},{192,0},{1,65},{65,129},{129,193},{193,1... | collective-permute-start | bytes 983048 | tf_op jit(solution)/shard_map/ppermute | solution.py:260
  123.3 8.9 %collective-permute-start.4 = (bf16[1280,128]{1,0:T(8,128)(2,1)S(1)}, bf16[1280,128]{1,0:T(8,128)(2,1)S(1)}, u32[]{:S(2)}, u32[]{:S(2)}) collective-permute-start(bf16[1280,128]{1,0:T(8,128)(2,1)S(1)} %slice.37), channel_id=1, source_target_pairs={{0,192},{64,0},{128,64},{192,128},{1,193},{65,1},{129,65},{193,129... | collective-permute-start | bytes 983048 | tf_op jit(solution)/shard_map/ppermute | solution.py:261
  137.7 8.0 %collective-permute-start.23 = (bf16[3,224,1024]{2,1,0:T(8,128)(2,1)S(1)}, bf16[3,224,1024]{2,1,0:T(8,128)(2,1)S(1)}, u32[]{:S(2)}, u32[]{:S(2)}) collective-permute-start(bf16[3,224,1024]{2,1,0:T(8,128)(2,1)S(1)} %get-tuple-element.8), channel_id=1, source_target_pairs={{0,1},{1,0},{2,3},{3,2},{4,5},{5,4},{6,7},{7,6},{8,9},{9,8},{10,11... | collective-permute-start | bytes 4128776 | tf_op jit(solution)/shard_map/ppermute | solution.py:293
  (5 other events, 15.9 us)

commit v2 on v1

--- a/solution.py
+++ b/solution.py
@@ -56,10 +56,9 @@
 CORE_SWAP = pairs_of(lambda x, z, c: (x, z, 1 - c))
 X_UP = pairs_of(lambda x, z, c: (x + 1, z, c))
 X_DOWN = pairs_of(lambda x, z, c: (x - 1, z, c))
+X_FAR = pairs_of(lambda x, z, c: (x + 2, z, c))
 Z_UP = pairs_of(lambda x, z, c: (x, z + 1, c))
 Z_DOWN = pairs_of(lambda x, z, c: (x, z - 1, c))
-Z_UP2 = pairs_of(lambda x, z, c: (x, z + 2, c))
-Z_DOWN2 = pairs_of(lambda x, z, c: (x, z - 2, c))
 Y_UP = [(y, (y + 1) % Y) for y in range(Y)]
 Y_DOWN = [(y, (y - 1) % Y) for y in range(Y)]
 XY_SWAP = [
@@ -70,8 +69,7 @@
     for c in range(C)
 ]
 XZ_GROUPS = [[place(x, z, c) for x in range(X) for z in range(Z)] for c in range(C)]
-PARCELS = ((0, -1, 1), (-2, -3, 2, 3), (4,))
-FAR_CUTS = (1, 2, 1)
+DISTANCES = (0, -1, 1, -2, 2, -3, 3, 4)
 VMEM = pl.BlockSpec(memory_space=pltpu.VMEM)
 SMEM = pl.BlockSpec(memory_space=pltpu.SMEM)
 
@@ -134,12 +132,8 @@
                 out_ref[x * Z + z, rows, :] = (mixed[x] * scale).astype(jnp.bfloat16)
 
 
-def partial_kernel(place_ref, r0, r1, r2a, r2b, r3, *refs):
-    refs, (own_ref, other_ref, lhs_ref) = list(refs[:-3]), refs[-3:]
-    grads = []
-    for parcel, cut in zip(PARCELS, FAR_CUTS):
-        grads.append([refs.pop(0) for _ in range(5 if cut < len(parcel) else 4)] + [None])
-        grads[-1] = grads[-1][:5]
+def partial_kernel(table, place_ref, r0, r1, r2a, r2b, r3, *refs):
+    grads, (own_ref, other_ref, lhs_ref) = refs[:-3], refs[-3:]
     core, shift, z_index = place_ref[0], place_ref[1], place_ref[2]
     half = own_ref.shape[1]
     tok = lhs_ref.shape[2]
@@ -166,17 +160,10 @@
             lhs_ref[s, slot, : tok // 2, 3 * LANES :] = last[:, : LANES // 2]
             lhs_ref[s, slot, tok // 2 :, 3 * LANES :] = last[:, LANES // 2 :]
 
-    spots = [(p, i) for p, parcel in enumerate(PARCELS) for i in range(len(parcel))]
-
     def piece(k, at, s):
-        p, i = spots[at]
-        whole, after, before, far_first, far_last = grads[p]
-        if k != 2:
-            return (whole, after, None, before)[k][i, s]
-        cut = FAR_CUTS[p]
-        return far_first[i, s] if i < cut else far_last[i - cut, s]
-
-    distances = [distance for parcel in PARCELS for distance in parcel]
+        array, index = table[DISTANCES[at]][k]
+        return grads[array][index, s]
+
     for s in range(SEQS):
         lhs = lhs_ref[s].reshape(Y * tok, 2 * half)
         for i in range(0, Z, 2):
@@ -191,7 +178,7 @@
                 lhs, rhs, (((0,), (0,)), ((), ())), preferred_element_type=jnp.float32
             )
             for at in range(2):
-                column = lax.rem(z_index + distances[i + at] + Z, Z)
+                column = lax.rem(z_index + DISTANCES[i + at] + Z, Z)
                 columns = pl.ds(pl.multiple_of(column * LANES, LANES), LANES)
                 low = both[:half, LANES * at : LANES * (at + 1)]
                 high = both[half:, LANES * at : LANES * (at + 1)]
@@ -262,25 +249,45 @@
 
     down1 = lax.ppermute(piece, "tensor", Z_UP)
     up1 = lax.ppermute(piece, "tensor", Z_DOWN)
-    down23 = lax.ppermute(jnp.stack([piece, down1]), "tensor", Z_UP2)
-    up23 = lax.ppermute(jnp.stack([piece, up1]), "tensor", Z_DOWN2)
-    down4 = lax.ppermute(down23[1:], "tensor", Z_UP)
-
-    grads = []
-
-    def along_x(block, cut):
+    down2 = lax.ppermute(down1, "tensor", Z_UP)
+    up2 = lax.ppermute(up1, "tensor", Z_DOWN)
+    down3 = lax.ppermute(down2, "tensor", Z_UP)
+    up3 = lax.ppermute(up2, "tensor", Z_DOWN)
+    down4 = lax.ppermute(down3, "tensor", Z_UP)
+
+    grads, table = [], {}
+
+    def keep(array):
+        grads.append(array)
+        return len(grads) - 1
+
+    def along_x(block, distances, cut):
         before = lax.ppermute(block, "tensor", X_UP)
         after = lax.ppermute(block, "tensor", X_DOWN)
-        grads.extend([block, after, before])
-        grads.append(lax.ppermute(before[:cut], "tensor", X_UP))
-        if cut < block.shape[0]:
-            grads.append(lax.ppermute(after[cut:], "tensor", X_DOWN))
-
-    along_x(jnp.stack([piece, down1, up1]), FAR_CUTS[0])
-    along_x(jnp.concatenate([down23, up23]), FAR_CUTS[1])
-    along_x(down4, FAR_CUTS[2])
+        fars = []
+        if cut:
+            far = lax.ppermute(before[:cut], "tensor", X_UP)
+            fars += [(keep(far), i) for i in range(cut)]
+        if cut is None:
+            far = keep(lax.ppermute(block, "tensor", X_FAR))
+            fars = [(far, i) for i in range(len(distances))]
+        elif cut < len(distances):
+            far = lax.ppermute(after[cut:], "tensor", X_DOWN)
+            fars += [(keep(far), i) for i in range(len(distances) - cut)]
+        spots = keep(block), keep(after), keep(before)
+        for i, distance in enumerate(distances):
+            table[distance] = ((spots[0], i), (spots[1], i), fars[i], (spots[2], i))
+
+    along_x(piece[None], (0,), 1)
+    others = jnp.concatenate([grads[array] for array, index in table[0][1:]])
+    for distance, near, pairs in ((-1, down1, Z_UP), (1, up1, Z_DOWN)):
+        rest = keep(lax.ppermute(others, "tensor", pairs))
+        table[distance] = ((keep(near[None]), 0), (rest, 0), (rest, 1), (rest, 2))
+    along_x(jnp.stack([down2, up2]), (-2, 2), 1)
+    along_x(jnp.stack([down3, up3]), (-3, 3), 1)
+    along_x(down4[None], (4,), None)
     own, sent = call(
-        partial_kernel,
+        lambda *refs: partial_kernel(table, *refs),
         (
             jax.ShapeDtypeStruct((seq_count, local_ff, features), jnp.float32),
             jax.ShapeDtypeStruct((seq_count, local_ff, features), jnp.bfloat16),

time: 147 us -> 144 us (0.980)
  local copies, waits for them, and re-layouts: 6.11 us -> 3.7 us
  starting transfers between devices: 70.3 us -> 68.7 us
    ppermute x1, waiting for transfers between devices: 1.05 us -> 18.2 us  [on_device(): down1 = lax.ppermute(piece, 'tensor', Z_UP)]
    ppermute x1, waiting for transfers between devices: 16 us -> 0.01 us  [on_device(): up1 = lax.ppermute(piece, 'tensor', Z_DOWN)]
    ppermute x3 -> x4, starting transfers between devices: 21.2 us -> 13.9 us  [along_x(): after = lax.ppermute(block, 'tensor', X_DOWN)]
    ppermute x1, starting transfers between devices: 5.2 us -> 9.77 us  [on_device(): got = lax.ppermute(sent, 'tensor', CORE_SWAP)]
    ppermute x1, starting transfers between devices: 4.87 us -> 1.68 us  [on_device(): far_high = lax.ppermute(above[cut:], 'dp', Y_DOWN)]
    ppermute x3 -> x4, waiting for transfers between devices: 1.88 us -> 4.99 us  [along_x(): after = lax.ppermute(block, 'tensor', X_DOWN)]
    ppermute x8 -> x13, waiting for transfers between devices: 12.9 us -> 10.1 us  [the longest x3 3.44 us: along_x(): far = lax.ppermute(before[:cut], 'tensor', X_UP)]
    ppermute x3 -> x4, starting transfers between devices: 0.78 us -> 3.07 us  [along_x(): before = lax.ppermute(block, 'tensor', X_UP)]
  transfers between devices with their start and end apart: 26 -> 33, of which waited for: 15 -> 11; matrix products, arithmetic and copies ran while one was open for 2% -> 1% of each run, Pallas kernels for 0% -> 1%
where the time goes in v2:
time: 144 us; the launch traced here: 143 us
  starting transfers between devices  68.7 us (48%)
  waiting for transfers between devices  59.5 us (41%)
  Pallas kernels  9.3 us (6%)
  local copies, waits for them, and re-layouts  3.7 us (3%)
    ppermute x1, waiting for transfers between devices, on_device(): down1 = lax.ppermute(piece, 'tensor', Z_UP)  18.2 us
    all_to_all x2, starting transfers between devices, exchange(): lax.all_to_all(array, 'tensor', split_axis=0, concat_axis=0, tiled=True,...  17.4 us
    all_to_all x2, waiting for transfers between devices, exchange(): lax.all_to_all(array, 'tensor', split_axis=0, concat_axis=0, tiled=True,...  15.7 us
    ppermute x4, starting transfers between devices, along_x(): after = lax.ppermute(block, 'tensor', X_DOWN)  13.9 us
    ppermute x1, starting transfers between devices, on_device(): got = lax.ppermute(sent, 'tensor', CORE_SWAP)  9.77 us
    ppermute x4, waiting for transfers between devices, along_x(): before = lax.ppermute(block, 'tensor', X_UP)  6.57 us
    ppermute x4, waiting for transfers between devices, along_x(): after = lax.ppermute(block, 'tensor', X_DOWN)  4.99 us
    pallas_call x1, Pallas kernels, on_device(): call(lambda *refs: partial_kernel(table, *refs), (jax.ShapeDtypeStruct((s...  4.79 us
  transfers between devices with their start and end apart: 33, of which 11 were waited for; matrix products, arithmetic and copies ran while one was open for 1% of the time, Pallas kernels for 1%

profile of v2, /device:TPU:1, one launch (start us, length us, event | category | flops | bytes accessed | tf_op | source)
XLA Modules:
  0.0 142.8 jit_solution(9916218131696222099)
XLA Ops:
  1.0 3.3 %collective-permute-start = (bf16[3,224,224]{2,1,0:T(8,128)(2,1)S(1)}, bf16[3,224,224]{2,1,0:T(8,128)(2,1)S(1)}, u32[]{:S(2)}, u32[]{:S(2)}) collective-permute-start(bf16[3,224,224]{2,1,0:T(8,128)(2,1)S(1)} %constant_dynamic-slice_fusion), channel_id=1, source_target_pairs={{0,1},{1,0},{2,3},{3,2},{4,5},{5,4},{6,7},{7,6},{8,9},{9,8},{10,11... | collective-permute-start | bytes 903176 | tf_op jit(solution)/shard_map/ppermute | solution.py:223
  7.7 2.0 %shard_map.37 = bf16[2560,128]{1,0:T(8,128)(2,1)} custom-call(s32[3]{0:T(128)S(1)} %pad_add_fusion.place_ref.refs_0_, bf16[3,448,224]{2,1,0:T(8,128)(2,1)S(1)} %copy-done, bf16[3,224,224]{2,1,0:T(8,128)(2,1)S(1)} %collective-permute-done.got_ref, bf16[2,224,448]{2,1,0:T(8,128)(2,1)S(1)} %copy-done.1), custom_call_target="tpu_custom_call" | custom-call | flops 269746176 | bytes 1048576 | tf_op jit(solution)/shard_map/pallas_call | solution.py:226
  9.7 9.3 %all-to-all-start = ((bf16[32,80,128]{2,1,0:T(8,128)(2,1)}), bf16[32,80,128]{2,1,0:T(8,128)(2,1)S(1)}, u32[]{:S(2)}, u32[]{:S(2)}) async-start(bf16[32,80,128]{2,1,0:T(8,128)(2,1)} %bitcast.3), calls=%async_computation | async-start | bytes 1310720 | tf_op jit(solution)/shard_map/all_to_all | solution.py:198
  20.2 15.7 %all-to-all-done.refs_0_ = bf16[32,80,128]{2,1,0:T(8,128)(2,1)S(1)} async-done(((bf16[32,80,128]{2,1,0:T(8,128)(2,1)}), bf16[32,80,128]{2,1,0:T(8,128)(2,1)S(1)}, u32[]{:S(2)}, u32[]{:S(2)}) %all-to-all-start) | async-done | bytes 655392 | tf_op jit(solution)/shard_map/all_to_all | solution.py:198
  37.1 8.1 %all-to-all-start.1 = ((bf16[32,80,128]{2,1,0:T(8,128)(2,1)}), bf16[32,80,128]{2,1,0:T(8,128)(2,1)S(1)}, u32[]{:S(2)}, u32[]{:S(2)}) async-start(bf16[32,80,128]{2,1,0:T(8,128)(2,1)} %shard_map.38), calls=%async_computation.1 | async-start | bytes 1310720 | tf_op jit(solution)/shard_map/all_to_all | solution.py:198
  47.4 18.2 %collective-permute-done.11 = bf16[3,224,128]{2,1,0:T(8,128)(2,1)S(1)} collective-permute-done((bf16[3,224,128]{2,1,0:T(8,128)(2,1)S(1)}, bf16[3,224,128]{2,1,0:T(8,128)(2,1)S(1)}, u32[]{:S(2)}, u32[]{:S(2)}) %collective-permute-start.11) | collective-permute-done | bytes 172064 | tf_op jit(solution)/shard_map/ppermute | solution.py:250
  65.6 2.7 %collective-permute-start.13 = (bf16[3,224,128]{2,1,0:T(8,128)(2,1)S(1)}, bf16[3,224,128]{2,1,0:T(8,128)(2,1)S(1)}, u32[]{:S(2)}, u32[]{:S(2)}) collective-permute-start(bf16[3,224,128]{2,1,0:T(8,128)(2,1)S(1)} %collective-permute-done.6), channel_id=1, source_target_pairs={{0,14},{1,15},{2,0},{3,1},{4,2},{5,3},{6,4},{7,5},{8,6},{9,7},{10,... | collective-permute-start | bytes 516104 | tf_op jit(solution)/shard_map/ppermute | solution.py:251
  71.1 2.7 %collective-permute-start.15 = (bf16[3,224,128]{2,1,0:T(8,128)(2,1)S(1)}, bf16[3,224,128]{2,1,0:T(8,128)(2,1)S(1)}, u32[]{:S(2)}, u32[]{:S(2)}) collective-permute-start(bf16[3,224,128]{2,1,0:T(8,128)(2,1)S(1)} %collective-permute-done.13), channel_id=1, source_target_pairs={{0,14},{1,15},{2,0},{3,1},{4,2},{5,3},{6,4},{7,5},{8,6},{9,7},{10,... | collective-permute-start | bytes 516104 | tf_op jit(solution)/shard_map/ppermute | solution.py:253
  73.7 8.1 %collective-permute-start.9 = (bf16[1,3,224,128]{3,2,1,0:T(8,128)(2,1)S(1)}, bf16[1,3,224,128]{3,2,1,0:T(8,128)(2,1)S(1)}, u32[]{:S(2)}, u32[]{:S(2)}) collective-permute-start(bf16[1,3,224,128]{3,2,1,0:T(8,128)(2,1)S(1)} %bitcast.17), channel_id=1, source_target_pairs={{0,48},{1,49},{2,50},{3,51},{4,52},{5,53},{6,54},{7,55},{8,56},{9,... | collective-permute-start | bytes 516104 | tf_op jit(solution)/shard_map/ppermute | solution.py:266
  82.0 2.8 %collective-permute-start.18 = (bf16[2,3,224,128]{3,2,1,0:T(8,128)(2,1)S(1)}, bf16[2,3,224,128]{3,2,1,0:T(8,128)(2,1)S(1)}, u32[]{:S(2)}, u32[]{:S(2)}) collective-permute-start(bf16[2,3,224,128]{3,2,1,0:T(8,128)(2,1)S(1)} %pad_maximum_fusion.refs_16_), channel_id=1, source_target_pairs={{0,48},{1,49},{2,50},{3,51},{4,52},{5,53},{6,54},{7,55},{8,56},{9,... | collective-permute-start | bytes 1032200 | tf_op jit(solution)/shard_map/ppermute | solution.py:266
  84.8 2.7 %collective-permute-start.21 = (bf16[3,224,128]{2,1,0:T(8,128)(2,1)S(1)}, bf16[3,224,128]{2,1,0:T(8,128)(2,1)}, u32[]{:S(2)}, u32[]{:S(2)}) collective-permute-start(bf16[3,224,128]{2,1,0:T(8,128)(2,1)S(1)} %collective-permute-done.15), channel_id=1, source_target_pairs={{0,14},{1,15},{2,0},{3,1},{4,2},{5,3},{6,4},{7,5},{8,6},{9,7},{10,... | collective-permute-start | bytes 516104 | tf_op jit(solution)/shard_map/ppermute | solution.py:255
  87.6 2.2 %collective-permute-done.21 = bf16[3,224,128]{2,1,0:T(8,128)(2,1)} collective-permute-done((bf16[3,224,128]{2,1,0:T(8,128)(2,1)S(1)}, bf16[3,224,128]{2,1,0:T(8,128)(2,1)}, u32[]{:S(2)}, u32[]{:S(2)}) %collective-permute-start.21) | collective-permute-done | bytes 172064 | tf_op jit(solution)/shard_map/ppermute | solution.py:255
  89.8 2.0 %collective-permute-start.1 = (bf16[2560,128]{1,0:T(8,128)(2,1)S(1)}, bf16[2560,128]{1,0:T(8,128)(2,1)S(1)}, u32[]{:S(2)}, u32[]{:S(2)}) collective-permute-start(bf16[2560,128]{1,0:T(8,128)(2,1)S(1)} %bitcast.14), channel_id=1, source_target_pairs={{0,192},{64,0},{128,64},{192,128},{1,193},{65,1},{129,65},{193,129... | collective-permute-start | bytes 1966088 | tf_op jit(solution)/shard_map/ppermute | solution.py:245
  92.7 2.0 %collective-permute-start.24 = (bf16[2,3,224,128]{3,2,1,0:T(8,128)(2,1)S(1)}, bf16[2,3,224,128]{3,2,1,0:T(8,128)(2,1)S(1)}, u32[]{:S(2)}, u32[]{:S(2)}) collective-permute-start(bf16[2,3,224,128]{3,2,1,0:T(8,128)(2,1)S(1)} %pad_maximum_fusion.1.refs_21_), channel_id=1, source_target_pairs={{0,48},{1,49},{2,50},{3,51},{4,52},{5,53},{6,54},{7,55},{8,56},{9,... | collective-permute-start | bytes 1032200 | tf_op jit(solution)/shard_map/ppermute | solution.py:266
  95.8 2.3 %collective-permute-done.29.refs_27_ = bf16[1,3,224,128]{3,2,1,0:T(8,128)(2,1)S(1)} collective-permute-done((bf16[1,3,224,128]{3,2,1,0:T(8,128)(2,1)S(1)}, bf16[1,3,224,128]{3,2,1,0:T(8,128)(2,1)S(1)}, u32[]{:S(2)}, u32[]{:S(2)}) %collective-permute-start.29) | collective-permute-done | bytes 172064 | tf_op jit(solution)/shard_map/ppermute | solution.py:265
  98.2 5.0 %collective-permute-done.28.refs_26_ = bf16[1,3,224,128]{3,2,1,0:T(8,128)(2,1)S(1)} collective-permute-done((bf16[1,3,224,128]{3,2,1,0:T(8,128)(2,1)S(1)}, bf16[1,3,224,128]{3,2,1,0:T(8,128)(2,1)S(1)}, u32[]{:S(2)}, u32[]{:S(2)}) %collective-permute-start.28) | collective-permute-done | bytes 172064 | tf_op jit(solution)/shard_map/ppermute | solution.py:266
  105.9 3.0 %collective-permute-start.19 = (bf16[1,3,224,128]{3,2,1,0:T(8,128)(2,1)S(1)}, bf16[1,3,224,128]{3,2,1,0:T(8,128)(2,1)S(1)}, u32[]{:S(2)}, u32[]{:S(2)}) collective-permute-start(bf16[1,3,224,128]{3,2,1,0:T(8,128)(2,1)S(1)} %slice.35), channel_id=1, source_target_pairs={{0,48},{1,49},{2,50},{3,51},{4,52},{5,53},{6,54},{7,55},{8,56},{9,... | collective-permute-start | bytes 516104 | tf_op jit(solution)/shard_map/ppermute | solution.py:275
  109.1 4.2 %collective-permute-done.22.refs_23_ = bf16[2,3,224,128]{3,2,1,0:T(8,128)(2,1)S(1)} collective-permute-done((bf16[2,3,224,128]{3,2,1,0:T(8,128)(2,1)S(1)}, bf16[2,3,224,128]{3,2,1,0:T(8,128)(2,1)S(1)}, u32[]{:S(2)}, u32[]{:S(2)}) %collective-permute-start.22) | collective-permute-done | bytes 344096 | tf_op jit(solution)/shard_map/ppermute | solution.py:265
  114.3 1.7 %collective-permute-start.4 = (bf16[1280,128]{1,0:T(8,128)(2,1)S(1)}, bf16[1280,128]{1,0:T(8,128)(2,1)S(1)}, u32[]{:S(2)}, u32[]{:S(2)}) collective-permute-start(bf16[1280,128]{1,0:T(8,128)(2,1)S(1)} %slice.33), channel_id=1, source_target_pairs={{0,192},{64,0},{128,64},{192,128},{1,193},{65,1},{129,65},{193,129... | collective-permute-start | bytes 983048 | tf_op jit(solution)/shard_map/ppermute | solution.py:248
  117.6 3.1 %collective-permute-done.25.refs_20_ = bf16[1,3,224,128]{3,2,1,0:T(8,128)(2,1)S(1)} collective-permute-done((bf16[1,3,224,128]{3,2,1,0:T(8,128)(2,1)S(1)}, bf16[1,3,224,128]{3,2,1,0:T(8,128)(2,1)S(1)}, u32[]{:S(2)}, u32[]{:S(2)}) %collective-permute-start.25) | collective-permute-done | bytes 172064 | tf_op jit(solution)/shard_map/ppermute | solution.py:275
  120.7 3.4 %collective-permute-done.23.refs_19_ = bf16[1,3,224,128]{3,2,1,0:T(8,128)(2,1)S(1)} collective-permute-done((bf16[1,3,224,128]{3,2,1,0:T(8,128)(2,1)S(1)}, bf16[1,3,224,128]{3,2,1,0:T(8,128)(2,1)S(1)}, u32[]{:S(2)}, u32[]{:S(2)}) %collective-permute-start.23) | collective-permute-done | bytes 172064 | tf_op jit(solution)/shard_map/ppermute | solution.py:269
  124.1 4.8 %shard_map.39 = (f32[3,224,1024]{2,1,0:T(8,128)S(1)}, bf16[3,224,1024]{2,1,0:T(8,128)(2,1)S(1)}) custom-call(s32[3]{0:T(128)S(1)} %pad_add_fusion.place_ref.refs_0_, bf16[2560,128]{1,0:T(8,128)(2,1)S(1)} %bitcast.15, bf16[2560,128]{1,0:T(8,128)(2,1)S(1)} %collective-permute-done.1.refs_2_, bf16[1280,128]{1,0:T(8,128)(2,1)S(1)} %collective-permute-done.3.refs_3_, ...), custom_call_target="tpu_custom_call" | custom-call | flops 2466250752 | bytes 1048576 | tf_op jit(solution)/shard_map/pallas_call | solution.py:289
  128.9 9.8 %collective-permute-start.30 = (bf16[3,224,1024]{2,1,0:T(8,128)(2,1)S(1)}, bf16[3,224,1024]{2,1,0:T(8,128)(2,1)S(1)}, u32[]{:S(2)}, u32[]{:S(2)}) collective-permute-start(bf16[3,224,1024]{2,1,0:T(8,128)(2,1)S(1)} %get-tuple-element.8), channel_id=1, source_target_pairs={{0,1},{1,0},{2,3},{3,2},{4,5},{5,4},{6,7},{7,6},{8,9},{9,8},{10,11... | collective-permute-start | bytes 4128776 | tf_op jit(solution)/shard_map/ppermute | solution.py:300
  138.7 2.8 %collective-permute-done.30.refs_1_ = bf16[3,224,1024]{2,1,0:T(8,128)(2,1)S(1)} collective-permute-done((bf16[3,224,1024]{2,1,0:T(8,128)(2,1)S(1)}, bf16[3,224,1024]{2,1,0:T(8,128)(2,1)S(1)}, u32[]{:S(2)}, u32[]{:S(2)}) %collective-permute-start.30) | collective-permute-done | bytes 1376288 | tf_op jit(solution)/shard_map/ppermute | solution.py:300
  (71 shorter events, 20.8 us)
Async XLA Ops:
  9.7 26.2 %all-to-all-start = ((bf16[32,80,128]{2,1,0:T(8,128)(2,1)}), bf16[32,80,128]{2,1,0:T(8,128)(2,1)S(1)}, u32[]{:S(2)}, u32[]{:S(2)}) async-start(bf16[32,80,128]{2,1,0:T(8,128)(2,1)} %bitcast.3), calls=%async_computation | async-start | bytes 1310720 | tf_op jit(solution)/shard_map/all_to_all | solution.py:198
  19.5 25.7 %collective-permute-start.5 = (bf16[3,224,64]{2,1,0:T(8,128)(2,1)S(1)}, bf16[3,224,64]{2,1,0:T(8,128)(2,1)S(1)}, u32[]{:S(2)}, u32[]{:S(2)}) collective-permute-start(bf16[3,224,64]{2,1,0:T(8,128)(2,1)S(1)} %broadcast_select_fusion.2), channel_id=1, source_target_pairs={{0,1},{1,0},{2,3},{3,2},{4,5},{5,4},{6,7},{7,6},{8,9},{9,8},{10,11... | collective-permute-start | bytes 258056 | tf_op jit(solution)/shard_map/ppermute | solution.py:218
  37.1 50.4 %all-to-all-start.1 = ((bf16[32,80,128]{2,1,0:T(8,128)(2,1)}), bf16[32,80,128]{2,1,0:T(8,128)(2,1)S(1)}, u32[]{:S(2)}, u32[]{:S(2)}) async-start(bf16[32,80,128]{2,1,0:T(8,128)(2,1)} %shard_map.38), calls=%async_computation.1 | async-start | bytes 1310720 | tf_op jit(solution)/shard_map/all_to_all | solution.py:198
  46.1 19.5 %collective-permute-start.11 = (bf16[3,224,128]{2,1,0:T(8,128)(2,1)S(1)}, bf16[3,224,128]{2,1,0:T(8,128)(2,1)S(1)}, u32[]{:S(2)}, u32[]{:S(2)}) collective-permute-start(bf16[3,224,128]{2,1,0:T(8,128)(2,1)S(1)} %collective-permute-done.6), channel_id=1, source_target_pairs={{0,2},{1,3},{2,4},{3,5},{4,6},{5,7},{6,8},{7,9},{8,10},{9,11},{10,... | collective-permute-start | bytes 516104 | tf_op jit(solution)/shard_map/ppermute | solution.py:250
  68.3 13.6 %collective-permute-start.7 = (bf16[1,3,224,128]{3,2,1,0:T(8,128)(2,1)S(1)}, bf16[1,3,224,128]{3,2,1,0:T(8,128)(2,1)S(1)}, u32[]{:S(2)}, u32[]{:S(2)}) collective-permute-start(bf16[1,3,224,128]{3,2,1,0:T(8,128)(2,1)S(1)} %bitcast.16), channel_id=1, source_target_pairs={{0,16},{1,17},{2,18},{3,19},{4,20},{5,21},{6,22},{7,23},{8,24},{9,... | collective-permute-start | bytes 516104 | tf_op jit(solution)/shard_map/ppermute | solution.py:265
  71.1 10.8 %collective-permute-start.20 = (bf16[3,224,128]{2,1,0:T(8,128)(2,1)S(1)}, bf16[3,224,128]{2,1,0:T(8,128)(2,1)S(1)}, u32[]{:S(2)}, u32[]{:S(2)}) collective-permute-start(bf16[3,224,128]{2,1,0:T(8,128)(2,1)S(1)} %collective-permute-done.14), channel_id=1, source_target_pairs={{0,2},{1,3},{2,4},{3,5},{4,6},{5,7},{6,8},{7,9},{8,10},{9,11},{10,... | collective-permute-start | bytes 516104 | tf_op jit(solution)/shard_map/ppermute | solution.py:254
  71.1 10.9 %collective-permute-start.15 = (bf16[3,224,128]{2,1,0:T(8,128)(2,1)S(1)}, bf16[3,224,128]{2,1,0:T(8,128)(2,1)S(1)}, u32[]{:S(2)}, u32[]{:S(2)}) collective-permute-start(bf16[3,224,128]{2,1,0:T(8,128)(2,1)S(1)} %collective-permute-done.13), channel_id=1, source_target_pairs={{0,14},{1,15},{2,0},{3,1},{4,2},{5,3},{6,4},{7,5},{8,6},{9,7},{10,... | collective-permute-start | bytes 516104 | tf_op jit(solution)/shard_map/ppermute | solution.py:253
  73.7 11.0 %collective-permute-start.9 = (bf16[1,3,224,128]{3,2,1,0:T(8,128)(2,1)S(1)}, bf16[1,3,224,128]{3,2,1,0:T(8,128)(2,1)S(1)}, u32[]{:S(2)}, u32[]{:S(2)}) collective-permute-start(bf16[1,3,224,128]{3,2,1,0:T(8,128)(2,1)S(1)} %bitcast.17), channel_id=1, source_target_pairs={{0,48},{1,49},{2,50},{3,51},{4,52},{5,53},{6,54},{7,55},{8,56},{9,... | collective-permute-start | bytes 516104 | tf_op jit(solution)/shard_map/ppermute | solution.py:266
  82.0 10.7 %collective-permute-start.18 = (bf16[2,3,224,128]{3,2,1,0:T(8,128)(2,1)S(1)}, bf16[2,3,224,128]{3,2,1,0:T(8,128)(2,1)S(1)}, u32[]{:S(2)}, u32[]{:S(2)}) collective-permute-start(bf16[2,3,224,128]{3,2,1,0:T(8,128)(2,1)S(1)} %pad_maximum_fusion.refs_16_), channel_id=1, source_target_pairs={{0,48},{1,49},{2,50},{3,51},{4,52},{5,53},{6,54},{7,55},{8,56},{9,... | collective-permute-start | bytes 1032200 | tf_op jit(solution)/shard_map/ppermute | solution.py:266
  84.8 10.0 %collective-permute-start.16 = (bf16[2,3,224,128]{3,2,1,0:T(8,128)(2,1)S(1)}, bf16[2,3,224,128]{3,2,1,0:T(8,128)(2,1)S(1)}, u32[]{:S(2)}, u32[]{:S(2)}) collective-permute-start(bf16[2,3,224,128]{3,2,1,0:T(8,128)(2,1)S(1)} %pad_maximum_fusion.refs_16_), channel_id=1, source_target_pairs={{0,16},{1,17},{2,18},{3,19},{4,20},{5,21},{6,22},{7,23},{8,24},{9,... | collective-permute-start | bytes 1032200 | tf_op jit(solution)/shard_map/ppermute | solution.py:265
  87.5 10.7 %collective-permute-start.29 = (bf16[1,3,224,128]{3,2,1,0:T(8,128)(2,1)S(1)}, bf16[1,3,224,128]{3,2,1,0:T(8,128)(2,1)S(1)}, u32[]{:S(2)}, u32[]{:S(2)}) collective-permute-start(bf16[1,3,224,128]{3,2,1,0:T(8,128)(2,1)S(1)} %bitcast.21), channel_id=1, source_target_pairs={{0,16},{1,17},{2,18},{3,19},{4,20},{5,21},{6,22},{7,23},{8,24},{9,... | collective-permute-start | bytes 516104 | tf_op jit(solution)/shard_map/ppermute | solution.py:265
  87.5 18.5 %collective-permute-start.2 = (bf16[2560,128]{1,0:T(8,128)(2,1)S(1)}, bf16[2560,128]{1,0:T(8,128)(2,1)S(1)}, u32[]{:S(2)}, u32[]{:S(2)}) collective-permute-start(bf16[2560,128]{1,0:T(8,128)(2,1)S(1)} %bitcast.13), channel_id=1, source_target_pairs={{0,64},{64,128},{128,192},{192,0},{1,65},{65,129},{129,193},{193,1... | collective-permute-start | bytes 1966088 | tf_op jit(solution)/shard_map/ppermute | solution.py:244
  89.8 19.1 %collective-permute-start.1 = (bf16[2560,128]{1,0:T(8,128)(2,1)S(1)}, bf16[2560,128]{1,0:T(8,128)(2,1)S(1)}, u32[]{:S(2)}, u32[]{:S(2)}) collective-permute-start(bf16[2560,128]{1,0:T(8,128)(2,1)S(1)} %bitcast.14), channel_id=1, source_target_pairs={{0,192},{64,0},{128,64},{192,128},{1,193},{65,1},{129,65},{193,129... | collective-permute-start | bytes 1966088 | tf_op jit(solution)/shard_map/ppermute | solution.py:245
  92.7 13.2 %collective-permute-start.24 = (bf16[2,3,224,128]{3,2,1,0:T(8,128)(2,1)S(1)}, bf16[2,3,224,128]{3,2,1,0:T(8,128)(2,1)S(1)}, u32[]{:S(2)}, u32[]{:S(2)}) collective-permute-start(bf16[2,3,224,128]{3,2,1,0:T(8,128)(2,1)S(1)} %pad_maximum_fusion.1.refs_21_), channel_id=1, source_target_pairs={{0,48},{1,49},{2,50},{3,51},{4,52},{5,53},{6,54},{7,55},{8,56},{9,... | collective-permute-start | bytes 1032200 | tf_op jit(solution)/shard_map/ppermute | solution.py:266
  94.8 8.4 %collective-permute-start.28 = (bf16[1,3,224,128]{3,2,1,0:T(8,128)(2,1)S(1)}, bf16[1,3,224,128]{3,2,1,0:T(8,128)(2,1)S(1)}, u32[]{:S(2)}, u32[]{:S(2)}) collective-permute-start(bf16[1,3,224,128]{3,2,1,0:T(8,128)(2,1)S(1)} %bitcast.22), channel_id=1, source_target_pairs={{0,48},{1,49},{2,50},{3,51},{4,52},{5,53},{6,54},{7,55},{8,56},{9,... | collective-permute-start | bytes 516104 | tf_op jit(solution)/shard_map/ppermute | solution.py:266
  103.2 14.4 %collective-permute-start.12 = (bf16[3,3,224,128]{3,2,1,0:T(8,128)(2,1)S(1)}, bf16[3,3,224,128]{3,2,1,0:T(8,128)(2,1)S(1)}, u32[]{:S(2)}, u32[]{:S(2)}) collective-permute-start(bf16[3,3,224,128]{3,2,1,0:T(8,128)(2,1)S(1)} %constant_dynamic-update-slice_fusion), channel_id=1, source_target_pairs={{0,14},{1,15},{2,0},{3,1},{4,2},{5,3},{6,4},{7,5},{8,6},{9,7},{10,... | collective-permute-start | bytes 1548296 | tf_op jit(solution)/shard_map/ppermute | solution.py:284
  104.3 9.0 %collective-permute-start.22 = (bf16[2,3,224,128]{3,2,1,0:T(8,128)(2,1)S(1)}, bf16[2,3,224,128]{3,2,1,0:T(8,128)(2,1)S(1)}, u32[]{:S(2)}, u32[]{:S(2)}) collective-permute-start(bf16[2,3,224,128]{3,2,1,0:T(8,128)(2,1)S(1)} %pad_maximum_fusion.1.refs_21_), channel_id=1, source_target_pairs={{0,16},{1,17},{2,18},{3,19},{4,20},{5,21},{6,22},{7,23},{8,24},{9,... | collective-permute-start | bytes 1032200 | tf_op jit(solution)/shard_map/ppermute | solution.py:265
  105.9 11.7 %collective-permute-start.10 = (bf16[3,3,224,128]{3,2,1,0:T(8,128)(2,1)S(1)}, bf16[3,3,224,128]{3,2,1,0:T(8,128)(2,1)S(1)}, u32[]{:S(2)}, u32[]{:S(2)}) collective-permute-start(bf16[3,3,224,128]{3,2,1,0:T(8,128)(2,1)S(1)} %constant_dynamic-update-slice_fusion), channel_id=1, source_target_pairs={{0,2},{1,3},{2,4},{3,5},{4,6},{5,7},{6,8},{7,9},{8,10},{9,11},{10,... | collective-permute-start | bytes 1548296 | tf_op jit(solution)/shard_map/ppermute | solution.py:284
  105.9 8.4 %collective-permute-start.19 = (bf16[1,3,224,128]{3,2,1,0:T(8,128)(2,1)S(1)}, bf16[1,3,224,128]{3,2,1,0:T(8,128)(2,1)S(1)}, u32[]{:S(2)}, u32[]{:S(2)}) collective-permute-start(bf16[1,3,224,128]{3,2,1,0:T(8,128)(2,1)S(1)} %slice.35), channel_id=1, source_target_pairs={{0,48},{1,49},{2,50},{3,51},{4,52},{5,53},{6,54},{7,55},{8,56},{9,... | collective-permute-start | bytes 516104 | tf_op jit(solution)/shard_map/ppermute | solution.py:275
  108.9 7.1 %collective-permute-start.17 = (bf16[1,3,224,128]{3,2,1,0:T(8,128)(2,1)S(1)}, bf16[1,3,224,128]{3,2,1,0:T(8,128)(2,1)S(1)}, u32[]{:S(2)}, u32[]{:S(2)}) collective-permute-start(bf16[1,3,224,128]{3,2,1,0:T(8,128)(2,1)S(1)} %slice.34), channel_id=1, source_target_pairs={{0,16},{1,17},{2,18},{3,19},{4,20},{5,21},{6,22},{7,23},{8,24},{9,... | collective-permute-start | bytes 516104 | tf_op jit(solution)/shard_map/ppermute | solution.py:269
  113.3 10.8 %collective-permute-start.3 = (bf16[1280,128]{1,0:T(8,128)(2,1)S(1)}, bf16[1280,128]{1,0:T(8,128)(2,1)S(1)}, u32[]{:S(2)}, u32[]{:S(2)}) collective-permute-start(bf16[1280,128]{1,0:T(8,128)(2,1)S(1)} %slice.32), channel_id=1, source_target_pairs={{0,64},{64,128},{128,192},{192,0},{1,65},{65,129},{129,193},{193,1... | collective-permute-start | bytes 983048 | tf_op jit(solution)/shard_map/ppermute | solution.py:247
  114.3 9.8 %collective-permute-start.4 = (bf16[1280,128]{1,0:T(8,128)(2,1)S(1)}, bf16[1280,128]{1,0:T(8,128)(2,1)S(1)}, u32[]{:S(2)}, u32[]{:S(2)}) collective-permute-start(bf16[1280,128]{1,0:T(8,128)(2,1)S(1)} %slice.33), channel_id=1, source_target_pairs={{0,192},{64,0},{128,64},{192,128},{1,193},{65,1},{129,65},{193,129... | collective-permute-start | bytes 983048 | tf_op jit(solution)/shard_map/ppermute | solution.py:248
  117.6 6.5 %collective-permute-start.23 = (bf16[1,3,224,128]{3,2,1,0:T(8,128)(2,1)S(1)}, bf16[1,3,224,128]{3,2,1,0:T(8,128)(2,1)S(1)}, u32[]{:S(2)}, u32[]{:S(2)}) collective-permute-start(bf16[1,3,224,128]{3,2,1,0:T(8,128)(2,1)S(1)} %slice.36), channel_id=1, source_target_pairs={{0,16},{1,17},{2,18},{3,19},{4,20},{5,21},{6,22},{7,23},{8,24},{9,... | collective-permute-start | bytes 516104 | tf_op jit(solution)/shard_map/ppermute | solution.py:269
  128.9 12.5 %collective-permute-start.30 = (bf16[3,224,1024]{2,1,0:T(8,128)(2,1)S(1)}, bf16[3,224,1024]{2,1,0:T(8,128)(2,1)S(1)}, u32[]{:S(2)}, u32[]{:S(2)}) collective-permute-start(bf16[3,224,1024]{2,1,0:T(8,128)(2,1)S(1)} %get-tuple-element.8), channel_id=1, source_target_pairs={{0,1},{1,0},{2,3},{3,2},{4,5},{5,4},{6,7},{7,6},{8,9},{9,8},{10,11... | collective-permute-start | bytes 4128776 | tf_op jit(solution)/shard_map/ppermute | solution.py:300
  (12 other events, 56.6 us)

commit v3 on v2

--- a/solution.py
+++ b/solution.py
@@ -132,40 +132,56 @@
                 out_ref[x * Z + z, rows, :] = (mixed[x] * scale).astype(jnp.bfloat16)
 
 
-def partial_kernel(table, place_ref, r0, r1, r2a, r2b, r3, *refs):
-    grads, (own_ref, other_ref, lhs_ref) = refs[:-3], refs[-3:]
+def unpack(packed, store):
+    tok = 224
+    rows = 7 * tok // 2
+    for s in range(SEQS):
+        for j in range(3):
+            columns = slice(LANES * j, LANES * (j + 1))
+            store(s, slice(0, tok), columns, packed(rows * s + tok * j, tok))
+        last = packed(rows * s + tok * 3, tok // 2)
+        columns = slice(3 * LANES, 3 * LANES + LANES // 2)
+        store(s, slice(0, tok // 2), columns, last[:, : LANES // 2])
+        store(s, slice(tok // 2, tok), columns, last[:, LANES // 2 :])
+
+
+def unpack_kernel(place_ref, r0, r1, r3, lhs_ref):
+    for d, ref in ((0, r0), (1, r1), (3, r3)):
+        slot = lax.rem(d - place_ref[1] + Y, Y)
+
+        def store(s, rows, columns, value):
+            lhs_ref[s, slot, rows, columns] = value
+
+        unpack(lambda start, count: ref[start : start + count, :], store)
+
+
+def partial_kernel(table, place_ref, early_ref, r2a, r2b, *refs):
+    grads, (own_ref, other_ref, far_ref) = refs[:-3], refs[-3:]
     core, shift, z_index = place_ref[0], place_ref[1], place_ref[2]
     half = own_ref.shape[1]
-    tok = lhs_ref.shape[2]
-    rows = 7 * tok // 2
     cut = r2a.shape[0]
-
-    def packed(d, start, count):
-        if d != 2:
-            return (r0, r1, None, r3)[d][start : start + count, :]
+    far_slot = lax.rem(2 - shift + Y, Y)
+
+    def packed(start, count):
         if start + count <= cut:
             return r2a[start : start + count, :]
         if start >= cut:
             return r2b[start - cut : start - cut + count, :]
         return jnp.concatenate([r2a[start:, :], r2b[: start + count - cut, :]], axis=0)
 
-    for d in range(Y):
-        slot = lax.rem(d - shift + Y, Y)
-        for s in range(SEQS):
-            for j in range(3):
-                lhs_ref[s, slot, :, LANES * j : LANES * (j + 1)] = packed(
-                    d, rows * s + tok * j, tok
-                )
-            last = packed(d, rows * s + tok * 3, tok // 2)
-            lhs_ref[s, slot, : tok // 2, 3 * LANES :] = last[:, : LANES // 2]
-            lhs_ref[s, slot, tok // 2 :, 3 * LANES :] = last[:, LANES // 2 :]
+    def store(s, rows, columns, value):
+        far_ref[s, rows, columns] = value
+
+    unpack(packed, store)
 
     def piece(k, at, s):
         array, index = table[DISTANCES[at]][k]
         return grads[array][index, s]
 
     for s in range(SEQS):
-        lhs = lhs_ref[s].reshape(Y * tok, 2 * half)
+        lhs = jnp.concatenate(
+            [jnp.where(far_slot == k, far_ref[s], early_ref[s, k]) for k in range(Y)], axis=0
+        )
         for i in range(0, Z, 2):
             rhs = jnp.concatenate(
                 [
@@ -286,17 +302,24 @@
     along_x(jnp.stack([down2, up2]), (-2, 2), 1)
     along_x(jnp.stack([down3, up3]), (-3, 3), 1)
     along_x(down4[None], (4,), None)
+    early = call(
+        unpack_kernel,
+        jax.ShapeDtypeStruct((seq_count, Y, half, width), jnp.bfloat16),
+        [SMEM, VMEM, VMEM, VMEM],
+        10**7,
+        16,
+    )(places, rotated, above, below)
     own, sent = call(
         lambda *refs: partial_kernel(table, *refs),
         (
             jax.ShapeDtypeStruct((seq_count, local_ff, features), jnp.float32),
             jax.ShapeDtypeStruct((seq_count, local_ff, features), jnp.bfloat16),
         ),
-        [SMEM] + [VMEM] * (5 + len(grads)),
+        [SMEM] + [VMEM] * (3 + len(grads)),
         2 * seq_count * half * Y * width * features,
         40,
-        [pltpu.VMEM((seq_count, Y, half, width), jnp.bfloat16)],
-    )(places, rotated, above, far_low, far_high, below, *grads)
+        [pltpu.VMEM((seq_count, half, width), jnp.bfloat16)],
+    )(places, early, far_low, far_high, *grads)
     got = lax.ppermute(sent, "tensor", CORE_SWAP)
     return call(
         lambda *refs: fisher_kernel(1.0 / (tok_rows * Y * SEQS), *refs),

time: 144 us -> 144 us (level)
  transfers between devices with their start and end apart: 33 -> 33, of which waited for: 11 -> 11; matrix products, arithmetic and copies ran while one was open for 1% -> 1% of each run, Pallas kernels for 1% -> 2%
where the time goes in v3:
time: 144 us; the launch traced here: 142 us
  starting transfers between devices  68.7 us (48%)
  waiting for transfers between devices  58.6 us (41%)
  Pallas kernels  9.83 us (7%)
  local copies, waits for them, and re-layouts  3.74 us (3%)
    ppermute x1, waiting for transfers between devices, on_device(): down1 = lax.ppermute(piece, 'tensor', Z_UP)  18.2 us
    all_to_all x2, starting transfers between devices, exchange(): lax.all_to_all(array, 'tensor', split_axis=0, concat_axis=0, tiled=True,...  17.4 us
    all_to_all x2, waiting for transfers between devices, exchange(): lax.all_to_all(array, 'tensor', split_axis=0, concat_axis=0, tiled=True,...  15.7 us
    ppermute x4, starting transfers between devices, along_x(): after = lax.ppermute(block, 'tensor', X_DOWN)  13.9 us
    ppermute x1, starting transfers between devices, on_device(): got = lax.ppermute(sent, 'tensor', CORE_SWAP)  9.76 us
    ppermute x4, waiting for transfers between devices, along_x(): before = lax.ppermute(block, 'tensor', X_UP)  6.58 us
    ppermute x4, waiting for transfers between devices, along_x(): after = lax.ppermute(block, 'tensor', X_DOWN)  4.99 us
    ppermute x2, starting transfers between devices, along_x(): far = lax.ppermute(after[cut:], 'tensor', X_DOWN)  4.49 us
  transfers between devices with their start and end apart: 33, of which 11 were waited for; matrix products, arithmetic and copies ran while one was open for 1% of the time, Pallas kernels for 2%

profile of v3, /device:TPU:1, one launch (start us, length us, event | category | flops | bytes accessed | tf_op | source)
XLA Modules:
  0.0 142.4 jit_solution(856593301086456381)
XLA Ops:
  1.0 3.3 %collective-permute-start = (bf16[3,224,224]{2,1,0:T(8,128)(2,1)S(1)}, bf16[3,224,224]{2,1,0:T(8,128)(2,1)S(1)}, u32[]{:S(2)}, u32[]{:S(2)}) collective-permute-start(bf16[3,224,224]{2,1,0:T(8,128)(2,1)S(1)} %constant_dynamic-slice_fusion), channel_id=1, source_target_pairs={{0,1},{1,0},{2,3},{3,2},{4,5},{5,4},{6,7},{7,6},{8,9},{9,8},{10,11... | collective-permute-start | bytes 903176 | tf_op jit(solution)/shard_map/ppermute | solution.py:239
  7.7 2.0 %shard_map.37 = bf16[2560,128]{1,0:T(8,128)(2,1)} custom-call(s32[3]{0:T(128)S(1)} %pad_add_fusion.place_ref.refs_0_, bf16[3,448,224]{2,1,0:T(8,128)(2,1)S(1)} %copy-done, bf16[3,224,224]{2,1,0:T(8,128)(2,1)S(1)} %collective-permute-done.got_ref, bf16[2,224,448]{2,1,0:T(8,128)(2,1)S(1)} %copy-done.1), custom_call_target="tpu_custom_call" | custom-call | flops 269746176 | bytes 1048576 | tf_op jit(solution)/shard_map/pallas_call | solution.py:242
  9.7 9.3 %all-to-all-start = ((bf16[32,80,128]{2,1,0:T(8,128)(2,1)}), bf16[32,80,128]{2,1,0:T(8,128)(2,1)S(1)}, u32[]{:S(2)}, u32[]{:S(2)}) async-start(bf16[32,80,128]{2,1,0:T(8,128)(2,1)} %bitcast.3), calls=%async_computation | async-start | bytes 1310720 | tf_op jit(solution)/shard_map/all_to_all | solution.py:214
  20.3 15.7 %all-to-all-done.refs_0_ = bf16[32,80,128]{2,1,0:T(8,128)(2,1)S(1)} async-done(((bf16[32,80,128]{2,1,0:T(8,128)(2,1)}), bf16[32,80,128]{2,1,0:T(8,128)(2,1)S(1)}, u32[]{:S(2)}, u32[]{:S(2)}) %all-to-all-start) | async-done | bytes 655392 | tf_op jit(solution)/shard_map/all_to_all | solution.py:214
  37.2 8.1 %all-to-all-start.1 = ((bf16[32,80,128]{2,1,0:T(8,128)(2,1)}), bf16[32,80,128]{2,1,0:T(8,128)(2,1)S(1)}, u32[]{:S(2)}, u32[]{:S(2)}) async-start(bf16[32,80,128]{2,1,0:T(8,128)(2,1)} %shard_map.38), calls=%async_computation.1 | async-start | bytes 1310720 | tf_op jit(solution)/shard_map/all_to_all | solution.py:214
  47.4 18.2 %collective-permute-done.11 = bf16[3,224,128]{2,1,0:T(8,128)(2,1)S(1)} collective-permute-done((bf16[3,224,128]{2,1,0:T(8,128)(2,1)S(1)}, bf16[3,224,128]{2,1,0:T(8,128)(2,1)S(1)}, u32[]{:S(2)}, u32[]{:S(2)}) %collective-permute-start.11) | collective-permute-done | bytes 172064 | tf_op jit(solution)/shard_map/ppermute | solution.py:266
  65.6 2.7 %collective-permute-start.13 = (bf16[3,224,128]{2,1,0:T(8,128)(2,1)S(1)}, bf16[3,224,128]{2,1,0:T(8,128)(2,1)S(1)}, u32[]{:S(2)}, u32[]{:S(2)}) collective-permute-start(bf16[3,224,128]{2,1,0:T(8,128)(2,1)S(1)} %collective-permute-done.6), channel_id=1, source_target_pairs={{0,14},{1,15},{2,0},{3,1},{4,2},{5,3},{6,4},{7,5},{8,6},{9,7},{10,... | collective-permute-start | bytes 516104 | tf_op jit(solution)/shard_map/ppermute | solution.py:267
  71.1 2.7 %collective-permute-start.15 = (bf16[3,224,128]{2,1,0:T(8,128)(2,1)S(1)}, bf16[3,224,128]{2,1,0:T(8,128)(2,1)S(1)}, u32[]{:S(2)}, u32[]{:S(2)}) collective-permute-start(bf16[3,224,128]{2,1,0:T(8,128)(2,1)S(1)} %collective-permute-done.13), channel_id=1, source_target_pairs={{0,14},{1,15},{2,0},{3,1},{4,2},{5,3},{6,4},{7,5},{8,6},{9,7},{10,... | collective-permute-start | bytes 516104 | tf_op jit(solution)/shard_map/ppermute | solution.py:269
  73.8 8.1 %collective-permute-start.9 = (bf16[1,3,224,128]{3,2,1,0:T(8,128)(2,1)S(1)}, bf16[1,3,224,128]{3,2,1,0:T(8,128)(2,1)S(1)}, u32[]{:S(2)}, u32[]{:S(2)}) collective-permute-start(bf16[1,3,224,128]{3,2,1,0:T(8,128)(2,1)S(1)} %bitcast.17), channel_id=1, source_target_pairs={{0,48},{1,49},{2,50},{3,51},{4,52},{5,53},{6,54},{7,55},{8,56},{9,... | collective-permute-start | bytes 516104 | tf_op jit(solution)/shard_map/ppermute | solution.py:282
  82.1 2.8 %collective-permute-start.18 = (bf16[2,3,224,128]{3,2,1,0:T(8,128)(2,1)S(1)}, bf16[2,3,224,128]{3,2,1,0:T(8,128)(2,1)S(1)}, u32[]{:S(2)}, u32[]{:S(2)}) collective-permute-start(bf16[2,3,224,128]{3,2,1,0:T(8,128)(2,1)S(1)} %pad_maximum_fusion.refs_14_), channel_id=1, source_target_pairs={{0,48},{1,49},{2,50},{3,51},{4,52},{5,53},{6,54},{7,55},{8,56},{9,... | collective-permute-start | bytes 1032200 | tf_op jit(solution)/shard_map/ppermute | solution.py:282
  84.8 2.7 %collective-permute-start.21 = (bf16[3,224,128]{2,1,0:T(8,128)(2,1)S(1)}, bf16[3,224,128]{2,1,0:T(8,128)(2,1)}, u32[]{:S(2)}, u32[]{:S(2)}) collective-permute-start(bf16[3,224,128]{2,1,0:T(8,128)(2,1)S(1)} %collective-permute-done.15), channel_id=1, source_target_pairs={{0,14},{1,15},{2,0},{3,1},{4,2},{5,3},{6,4},{7,5},{8,6},{9,7},{10,... | collective-permute-start | bytes 516104 | tf_op jit(solution)/shard_map/ppermute | solution.py:271
  87.6 2.2 %collective-permute-done.21 = bf16[3,224,128]{2,1,0:T(8,128)(2,1)} collective-permute-done((bf16[3,224,128]{2,1,0:T(8,128)(2,1)S(1)}, bf16[3,224,128]{2,1,0:T(8,128)(2,1)}, u32[]{:S(2)}, u32[]{:S(2)}) %collective-permute-start.21) | collective-permute-done | bytes 172064 | tf_op jit(solution)/shard_map/ppermute | solution.py:271
  89.9 2.0 %collective-permute-start.1 = (bf16[2560,128]{1,0:T(8,128)(2,1)S(1)}, bf16[2560,128]{1,0:T(8,128)(2,1)S(1)}, u32[]{:S(2)}, u32[]{:S(2)}) collective-permute-start(bf16[2560,128]{1,0:T(8,128)(2,1)S(1)} %bitcast.14), channel_id=1, source_target_pairs={{0,192},{64,0},{128,64},{192,128},{1,193},{65,1},{129,65},{193,129... | collective-permute-start | bytes 1966088 | tf_op jit(solution)/shard_map/ppermute | solution.py:261
  92.8 2.0 %collective-permute-start.24 = (bf16[2,3,224,128]{3,2,1,0:T(8,128)(2,1)S(1)}, bf16[2,3,224,128]{3,2,1,0:T(8,128)(2,1)S(1)}, u32[]{:S(2)}, u32[]{:S(2)}) collective-permute-start(bf16[2,3,224,128]{3,2,1,0:T(8,128)(2,1)S(1)} %pad_maximum_fusion.1.refs_19_), channel_id=1, source_target_pairs={{0,48},{1,49},{2,50},{3,51},{4,52},{5,53},{6,54},{7,55},{8,56},{9,... | collective-permute-start | bytes 1032200 | tf_op jit(solution)/shard_map/ppermute | solution.py:282
  95.8 2.3 %collective-permute-done.29.refs_25_ = bf16[1,3,224,128]{3,2,1,0:T(8,128)(2,1)S(1)} collective-permute-done((bf16[1,3,224,128]{3,2,1,0:T(8,128)(2,1)S(1)}, bf16[1,3,224,128]{3,2,1,0:T(8,128)(2,1)S(1)}, u32[]{:S(2)}, u32[]{:S(2)}) %collective-permute-start.29) | collective-permute-done | bytes 172064 | tf_op jit(solution)/shard_map/ppermute | solution.py:281
  98.2 5.0 %collective-permute-done.28.refs_24_ = bf16[1,3,224,128]{3,2,1,0:T(8,128)(2,1)S(1)} collective-permute-done((bf16[1,3,224,128]{3,2,1,0:T(8,128)(2,1)S(1)}, bf16[1,3,224,128]{3,2,1,0:T(8,128)(2,1)S(1)}, u32[]{:S(2)}, u32[]{:S(2)}) %collective-permute-start.28) | collective-permute-done | bytes 172064 | tf_op jit(solution)/shard_map/ppermute | solution.py:282
  106.0 3.0 %collective-permute-start.19 = (bf16[1,3,224,128]{3,2,1,0:T(8,128)(2,1)S(1)}, bf16[1,3,224,128]{3,2,1,0:T(8,128)(2,1)S(1)}, u32[]{:S(2)}, u32[]{:S(2)}) collective-permute-start(bf16[1,3,224,128]{3,2,1,0:T(8,128)(2,1)S(1)} %slice.35), channel_id=1, source_target_pairs={{0,48},{1,49},{2,50},{3,51},{4,52},{5,53},{6,54},{7,55},{8,56},{9,... | collective-permute-start | bytes 516104 | tf_op jit(solution)/shard_map/ppermute | solution.py:291
  109.1 4.2 %collective-permute-done.22.refs_21_ = bf16[2,3,224,128]{3,2,1,0:T(8,128)(2,1)S(1)} collective-permute-done((bf16[2,3,224,128]{3,2,1,0:T(8,128)(2,1)S(1)}, bf16[2,3,224,128]{3,2,1,0:T(8,128)(2,1)S(1)}, u32[]{:S(2)}, u32[]{:S(2)}) %collective-permute-start.22) | collective-permute-done | bytes 344096 | tf_op jit(solution)/shard_map/ppermute | solution.py:281
  114.4 1.7 %collective-permute-start.4 = (bf16[1280,128]{1,0:T(8,128)(2,1)S(1)}, bf16[1280,128]{1,0:T(8,128)(2,1)S(1)}, u32[]{:S(2)}, u32[]{:S(2)}) collective-permute-start(bf16[1280,128]{1,0:T(8,128)(2,1)S(1)} %slice.33), channel_id=1, source_target_pairs={{0,192},{64,0},{128,64},{192,128},{1,193},{65,1},{129,65},{193,129... | collective-permute-start | bytes 983048 | tf_op jit(solution)/shard_map/ppermute | solution.py:264
  118.6 2.1 %collective-permute-done.25.refs_18_ = bf16[1,3,224,128]{3,2,1,0:T(8,128)(2,1)S(1)} collective-permute-done((bf16[1,3,224,128]{3,2,1,0:T(8,128)(2,1)S(1)}, bf16[1,3,224,128]{3,2,1,0:T(8,128)(2,1)S(1)}, u32[]{:S(2)}, u32[]{:S(2)}) %collective-permute-start.25) | collective-permute-done | bytes 172064 | tf_op jit(solution)/shard_map/ppermute | solution.py:291
  120.7 3.4 %collective-permute-done.23.refs_17_ = bf16[1,3,224,128]{3,2,1,0:T(8,128)(2,1)S(1)} collective-permute-done((bf16[1,3,224,128]{3,2,1,0:T(8,128)(2,1)S(1)}, bf16[1,3,224,128]{3,2,1,0:T(8,128)(2,1)S(1)}, u32[]{:S(2)}, u32[]{:S(2)}) %collective-permute-start.23) | collective-permute-done | bytes 172064 | tf_op jit(solution)/shard_map/ppermute | solution.py:285
  124.2 4.4 %shard_map.40 = (f32[3,224,1024]{2,1,0:T(8,128)S(1)}, bf16[3,224,1024]{2,1,0:T(8,128)(2,1)S(1)}) custom-call(s32[3]{0:T(128)S(1)} %pad_add_fusion.place_ref.refs_0_, bf16[3,4,224,448]{3,2,1,0:T(8,128)(2,1)S(1)} %shard_map.39.refs_1_, bf16[1280,128]{1,0:T(8,128)(2,1)S(1)} %collective-permute-done.3.refs_2_, ...), custom_call_target="tpu_custom_call" | custom-call | flops 2466250752 | bytes 1048576 | tf_op jit(solution)/shard_map/pallas_call | solution.py:312
  128.6 9.8 %collective-permute-start.30 = (bf16[3,224,1024]{2,1,0:T(8,128)(2,1)S(1)}, bf16[3,224,1024]{2,1,0:T(8,128)(2,1)S(1)}, u32[]{:S(2)}, u32[]{:S(2)}) collective-permute-start(bf16[3,224,1024]{2,1,0:T(8,128)(2,1)S(1)} %get-tuple-element.8), channel_id=1, source_target_pairs={{0,1},{1,0},{2,3},{3,2},{4,5},{5,4},{6,7},{7,6},{8,9},{9,8},{10,11... | collective-permute-start | bytes 4128776 | tf_op jit(solution)/shard_map/ppermute | solution.py:323
  138.3 2.8 %collective-permute-done.30.refs_1_ = bf16[3,224,1024]{2,1,0:T(8,128)(2,1)S(1)} collective-permute-done((bf16[3,224,1024]{2,1,0:T(8,128)(2,1)S(1)}, bf16[3,224,1024]{2,1,0:T(8,128)(2,1)S(1)}, u32[]{:S(2)}, u32[]{:S(2)}) %collective-permute-start.30) | collective-permute-done | bytes 1376288 | tf_op jit(solution)/shard_map/ppermute | solution.py:323
  (72 shorter events, 21.8 us)
Async XLA Ops:
  9.7 26.3 %all-to-all-start = ((bf16[32,80,128]{2,1,0:T(8,128)(2,1)}), bf16[32,80,128]{2,1,0:T(8,128)(2,1)S(1)}, u32[]{:S(2)}, u32[]{:S(2)}) async-start(bf16[32,80,128]{2,1,0:T(8,128)(2,1)} %bitcast.3), calls=%async_computation | async-start | bytes 1310720 | tf_op jit(solution)/shard_map/all_to_all | solution.py:214
  19.5 25.7 %collective-permute-start.5 = (bf16[3,224,64]{2,1,0:T(8,128)(2,1)S(1)}, bf16[3,224,64]{2,1,0:T(8,128)(2,1)S(1)}, u32[]{:S(2)}, u32[]{:S(2)}) collective-permute-start(bf16[3,224,64]{2,1,0:T(8,128)(2,1)S(1)} %broadcast_select_fusion.2), channel_id=1, source_target_pairs={{0,1},{1,0},{2,3},{3,2},{4,5},{5,4},{6,7},{7,6},{8,9},{9,8},{10,11... | collective-permute-start | bytes 258056 | tf_op jit(solution)/shard_map/ppermute | solution.py:234
  37.2 50.4 %all-to-all-start.1 = ((bf16[32,80,128]{2,1,0:T(8,128)(2,1)}), bf16[32,80,128]{2,1,0:T(8,128)(2,1)S(1)}, u32[]{:S(2)}, u32[]{:S(2)}) async-start(bf16[32,80,128]{2,1,0:T(8,128)(2,1)} %shard_map.38), calls=%async_computation.1 | async-start | bytes 1310720 | tf_op jit(solution)/shard_map/all_to_all | solution.py:214
  46.1 19.5 %collective-permute-start.11 = (bf16[3,224,128]{2,1,0:T(8,128)(2,1)S(1)}, bf16[3,224,128]{2,1,0:T(8,128)(2,1)S(1)}, u32[]{:S(2)}, u32[]{:S(2)}) collective-permute-start(bf16[3,224,128]{2,1,0:T(8,128)(2,1)S(1)} %collective-permute-done.6), channel_id=1, source_target_pairs={{0,2},{1,3},{2,4},{3,5},{4,6},{5,7},{6,8},{7,9},{8,10},{9,11},{10,... | collective-permute-start | bytes 516104 | tf_op jit(solution)/shard_map/ppermute | solution.py:266
  68.3 13.6 %collective-permute-start.7 = (bf16[1,3,224,128]{3,2,1,0:T(8,128)(2,1)S(1)}, bf16[1,3,224,128]{3,2,1,0:T(8,128)(2,1)S(1)}, u32[]{:S(2)}, u32[]{:S(2)}) collective-permute-start(bf16[1,3,224,128]{3,2,1,0:T(8,128)(2,1)S(1)} %bitcast.16), channel_id=1, source_target_pairs={{0,16},{1,17},{2,18},{3,19},{4,20},{5,21},{6,22},{7,23},{8,24},{9,... | collective-permute-start | bytes 516104 | tf_op jit(solution)/shard_map/ppermute | solution.py:281
  71.1 10.8 %collective-permute-start.20 = (bf16[3,224,128]{2,1,0:T(8,128)(2,1)S(1)}, bf16[3,224,128]{2,1,0:T(8,128)(2,1)S(1)}, u32[]{:S(2)}, u32[]{:S(2)}) collective-permute-start(bf16[3,224,128]{2,1,0:T(8,128)(2,1)S(1)} %collective-permute-done.14), channel_id=1, source_target_pairs={{0,2},{1,3},{2,4},{3,5},{4,6},{5,7},{6,8},{7,9},{8,10},{9,11},{10,... | collective-permute-start | bytes 516104 | tf_op jit(solution)/shard_map/ppermute | solution.py:270
  71.1 10.9 %collective-permute-start.15 = (bf16[3,224,128]{2,1,0:T(8,128)(2,1)S(1)}, bf16[3,224,128]{2,1,0:T(8,128)(2,1)S(1)}, u32[]{:S(2)}, u32[]{:S(2)}) collective-permute-start(bf16[3,224,128]{2,1,0:T(8,128)(2,1)S(1)} %collective-permute-done.13), channel_id=1, source_target_pairs={{0,14},{1,15},{2,0},{3,1},{4,2},{5,3},{6,4},{7,5},{8,6},{9,7},{10,... | collective-permute-start | bytes 516104 | tf_op jit(solution)/shard_map/ppermute | solution.py:269
  73.8 11.1 %collective-permute-start.9 = (bf16[1,3,224,128]{3,2,1,0:T(8,128)(2,1)S(1)}, bf16[1,3,224,128]{3,2,1,0:T(8,128)(2,1)S(1)}, u32[]{:S(2)}, u32[]{:S(2)}) collective-permute-start(bf16[1,3,224,128]{3,2,1,0:T(8,128)(2,1)S(1)} %bitcast.17), channel_id=1, source_target_pairs={{0,48},{1,49},{2,50},{3,51},{4,52},{5,53},{6,54},{7,55},{8,56},{9,... | collective-permute-start | bytes 516104 | tf_op jit(solution)/shard_map/ppermute | solution.py:282
  82.1 10.7 %collective-permute-start.18 = (bf16[2,3,224,128]{3,2,1,0:T(8,128)(2,1)S(1)}, bf16[2,3,224,128]{3,2,1,0:T(8,128)(2,1)S(1)}, u32[]{:S(2)}, u32[]{:S(2)}) collective-permute-start(bf16[2,3,224,128]{3,2,1,0:T(8,128)(2,1)S(1)} %pad_maximum_fusion.refs_14_), channel_id=1, source_target_pairs={{0,48},{1,49},{2,50},{3,51},{4,52},{5,53},{6,54},{7,55},{8,56},{9,... | collective-permute-start | bytes 1032200 | tf_op jit(solution)/shard_map/ppermute | solution.py:282
  84.8 10.0 %collective-permute-start.16 = (bf16[2,3,224,128]{3,2,1,0:T(8,128)(2,1)S(1)}, bf16[2,3,224,128]{3,2,1,0:T(8,128)(2,1)S(1)}, u32[]{:S(2)}, u32[]{:S(2)}) collective-permute-start(bf16[2,3,224,128]{3,2,1,0:T(8,128)(2,1)S(1)} %pad_maximum_fusion.refs_14_), channel_id=1, source_target_pairs={{0,16},{1,17},{2,18},{3,19},{4,20},{5,21},{6,22},{7,23},{8,24},{9,... | collective-permute-start | bytes 1032200 | tf_op jit(solution)/shard_map/ppermute | solution.py:281
  87.5 10.7 %collective-permute-start.29 = (bf16[1,3,224,128]{3,2,1,0:T(8,128)(2,1)S(1)}, bf16[1,3,224,128]{3,2,1,0:T(8,128)(2,1)S(1)}, u32[]{:S(2)}, u32[]{:S(2)}) collective-permute-start(bf16[1,3,224,128]{3,2,1,0:T(8,128)(2,1)S(1)} %bitcast.21), channel_id=1, source_target_pairs={{0,16},{1,17},{2,18},{3,19},{4,20},{5,21},{6,22},{7,23},{8,24},{9,... | collective-permute-start | bytes 516104 | tf_op jit(solution)/shard_map/ppermute | solution.py:281
  87.5 18.5 %collective-permute-start.2 = (bf16[2560,128]{1,0:T(8,128)(2,1)S(1)}, bf16[2560,128]{1,0:T(8,128)(2,1)S(1)}, u32[]{:S(2)}, u32[]{:S(2)}) collective-permute-start(bf16[2560,128]{1,0:T(8,128)(2,1)S(1)} %bitcast.13), channel_id=1, source_target_pairs={{0,64},{64,128},{128,192},{192,0},{1,65},{65,129},{129,193},{193,1... | collective-permute-start | bytes 1966088 | tf_op jit(solution)/shard_map/ppermute | solution.py:260
  89.9 19.1 %collective-permute-start.1 = (bf16[2560,128]{1,0:T(8,128)(2,1)S(1)}, bf16[2560,128]{1,0:T(8,128)(2,1)S(1)}, u32[]{:S(2)}, u32[]{:S(2)}) collective-permute-start(bf16[2560,128]{1,0:T(8,128)(2,1)S(1)} %bitcast.14), channel_id=1, source_target_pairs={{0,192},{64,0},{128,64},{192,128},{1,193},{65,1},{129,65},{193,129... | collective-permute-start | bytes 1966088 | tf_op jit(solution)/shard_map/ppermute | solution.py:261
  92.8 13.2 %collective-permute-start.24 = (bf16[2,3,224,128]{3,2,1,0:T(8,128)(2,1)S(1)}, bf16[2,3,224,128]{3,2,1,0:T(8,128)(2,1)S(1)}, u32[]{:S(2)}, u32[]{:S(2)}) collective-permute-start(bf16[2,3,224,128]{3,2,1,0:T(8,128)(2,1)S(1)} %pad_maximum_fusion.1.refs_19_), channel_id=1, source_target_pairs={{0,48},{1,49},{2,50},{3,51},{4,52},{5,53},{6,54},{7,55},{8,56},{9,... | collective-permute-start | bytes 1032200 | tf_op jit(solution)/shard_map/ppermute | solution.py:282
  94.8 8.4 %collective-permute-start.28 = (bf16[1,3,224,128]{3,2,1,0:T(8,128)(2,1)S(1)}, bf16[1,3,224,128]{3,2,1,0:T(8,128)(2,1)S(1)}, u32[]{:S(2)}, u32[]{:S(2)}) collective-permute-start(bf16[1,3,224,128]{3,2,1,0:T(8,128)(2,1)S(1)} %bitcast.22), channel_id=1, source_target_pairs={{0,48},{1,49},{2,50},{3,51},{4,52},{5,53},{6,54},{7,55},{8,56},{9,... | collective-permute-start | bytes 516104 | tf_op jit(solution)/shard_map/ppermute | solution.py:282
  103.2 14.4 %collective-permute-start.12 = (bf16[3,3,224,128]{3,2,1,0:T(8,128)(2,1)S(1)}, bf16[3,3,224,128]{3,2,1,0:T(8,128)(2,1)S(1)}, u32[]{:S(2)}, u32[]{:S(2)}) collective-permute-start(bf16[3,3,224,128]{3,2,1,0:T(8,128)(2,1)S(1)} %constant_dynamic-update-slice_fusion), channel_id=1, source_target_pairs={{0,14},{1,15},{2,0},{3,1},{4,2},{5,3},{6,4},{7,5},{8,6},{9,7},{10,... | collective-permute-start | bytes 1548296 | tf_op jit(solution)/shard_map/ppermute | solution.py:300
  104.3 9.0 %collective-permute-start.22 = (bf16[2,3,224,128]{3,2,1,0:T(8,128)(2,1)S(1)}, bf16[2,3,224,128]{3,2,1,0:T(8,128)(2,1)S(1)}, u32[]{:S(2)}, u32[]{:S(2)}) collective-permute-start(bf16[2,3,224,128]{3,2,1,0:T(8,128)(2,1)S(1)} %pad_maximum_fusion.1.refs_19_), channel_id=1, source_target_pairs={{0,16},{1,17},{2,18},{3,19},{4,20},{5,21},{6,22},{7,23},{8,24},{9,... | collective-permute-start | bytes 1032200 | tf_op jit(solution)/shard_map/ppermute | solution.py:281
  106.0 12.6 %collective-permute-start.10 = (bf16[3,3,224,128]{3,2,1,0:T(8,128)(2,1)S(1)}, bf16[3,3,224,128]{3,2,1,0:T(8,128)(2,1)S(1)}, u32[]{:S(2)}, u32[]{:S(2)}) collective-permute-start(bf16[3,3,224,128]{3,2,1,0:T(8,128)(2,1)S(1)} %constant_dynamic-update-slice_fusion), channel_id=1, source_target_pairs={{0,2},{1,3},{2,4},{3,5},{4,6},{5,7},{6,8},{7,9},{8,10},{9,11},{10,... | collective-permute-start | bytes 1548296 | tf_op jit(solution)/shard_map/ppermute | solution.py:300
  106.0 8.4 %collective-permute-start.19 = (bf16[1,3,224,128]{3,2,1,0:T(8,128)(2,1)S(1)}, bf16[1,3,224,128]{3,2,1,0:T(8,128)(2,1)S(1)}, u32[]{:S(2)}, u32[]{:S(2)}) collective-permute-start(bf16[1,3,224,128]{3,2,1,0:T(8,128)(2,1)S(1)} %slice.35), channel_id=1, source_target_pairs={{0,48},{1,49},{2,50},{3,51},{4,52},{5,53},{6,54},{7,55},{8,56},{9,... | collective-permute-start | bytes 516104 | tf_op jit(solution)/shard_map/ppermute | solution.py:291
  109.0 7.1 %collective-permute-start.17 = (bf16[1,3,224,128]{3,2,1,0:T(8,128)(2,1)S(1)}, bf16[1,3,224,128]{3,2,1,0:T(8,128)(2,1)S(1)}, u32[]{:S(2)}, u32[]{:S(2)}) collective-permute-start(bf16[1,3,224,128]{3,2,1,0:T(8,128)(2,1)S(1)} %slice.34), channel_id=1, source_target_pairs={{0,16},{1,17},{2,18},{3,19},{4,20},{5,21},{6,22},{7,23},{8,24},{9,... | collective-permute-start | bytes 516104 | tf_op jit(solution)/shard_map/ppermute | solution.py:285
  113.4 10.8 %collective-permute-start.3 = (bf16[1280,128]{1,0:T(8,128)(2,1)S(1)}, bf16[1280,128]{1,0:T(8,128)(2,1)S(1)}, u32[]{:S(2)}, u32[]{:S(2)}) collective-permute-start(bf16[1280,128]{1,0:T(8,128)(2,1)S(1)} %slice.32), channel_id=1, source_target_pairs={{0,64},{64,128},{128,192},{192,0},{1,65},{65,129},{129,193},{193,1... | collective-permute-start | bytes 983048 | tf_op jit(solution)/shard_map/ppermute | solution.py:263
  114.4 9.8 %collective-permute-start.4 = (bf16[1280,128]{1,0:T(8,128)(2,1)S(1)}, bf16[1280,128]{1,0:T(8,128)(2,1)S(1)}, u32[]{:S(2)}, u32[]{:S(2)}) collective-permute-start(bf16[1280,128]{1,0:T(8,128)(2,1)S(1)} %slice.33), channel_id=1, source_target_pairs={{0,192},{64,0},{128,64},{192,128},{1,193},{65,1},{129,65},{193,129... | collective-permute-start | bytes 983048 | tf_op jit(solution)/shard_map/ppermute | solution.py:264
  117.6 6.5 %collective-permute-start.23 = (bf16[1,3,224,128]{3,2,1,0:T(8,128)(2,1)S(1)}, bf16[1,3,224,128]{3,2,1,0:T(8,128)(2,1)S(1)}, u32[]{:S(2)}, u32[]{:S(2)}) collective-permute-start(bf16[1,3,224,128]{3,2,1,0:T(8,128)(2,1)S(1)} %slice.36), channel_id=1, source_target_pairs={{0,16},{1,17},{2,18},{3,19},{4,20},{5,21},{6,22},{7,23},{8,24},{9,... | collective-permute-start | bytes 516104 | tf_op jit(solution)/shard_map/ppermute | solution.py:285
  128.6 12.5 %collective-permute-start.30 = (bf16[3,224,1024]{2,1,0:T(8,128)(2,1)S(1)}, bf16[3,224,1024]{2,1,0:T(8,128)(2,1)S(1)}, u32[]{:S(2)}, u32[]{:S(2)}) collective-permute-start(bf16[3,224,1024]{2,1,0:T(8,128)(2,1)S(1)} %get-tuple-element.8), channel_id=1, source_target_pairs={{0,1},{1,0},{2,3},{3,2},{4,5},{5,4},{6,7},{7,6},{8,9},{9,8},{10,11... | collective-permute-start | bytes 4128776 | tf_op jit(solution)/shard_map/ppermute | solution.py:323
  (12 other events, 64.3 us)
